TPU v7x, 8 devices: a whole 2x2x1 slice. The times are simulated.
8 devices in a mesh: pp: 4 (over z, y, x), ep: 2 (over core).
Axes of the slice: x: 2, y: 2, z: 1, core: 2. Of those that a mesh axis runs over, the one named last changes fastest.
Arguments:
- expert_out: bfloat16 [24, 8, 320, 4096], P('pp', 'ep')
- expert_ids: int32 [24, 2, 512, 2], P('pp', 'ep')
- slot_ids: int32 [24, 2, 512, 2], P('pp', 'ep')
- gate_vals: float32 [24, 2, 512, 2], P('pp', 'ep')
- residual: bfloat16 [24, 2, 512, 4096], P('pp', 'ep')
- norm_w: float32 [4, 4096], P('pp')
- w_query: bfloat16 [4, 4096, 32, 128], P('pp')
- w_key: bfloat16 [4, 4096, 32, 128], P('pp')
- w_value: bfloat16 [4, 4096, 32, 128], P('pp')
- w_out: bfloat16 [4, 32, 128, 4096], P('pp')
Outputs:
- output: bfloat16 [24, 2, 512, 4096], P('pp', 'ep')
All inputs are finite; a program needn't handle non-finite values.
Results may differ from a plain program's by a relative error of at most 0.0114582.
Values are sent between devices in bfloat16 or wider.
A program may use at most 1 GiB of HBM per device.

v0:
```python
import jax
import jax.numpy as jnp
from jax import lax
from jax.sharding import PartitionSpec as P

NORM_EPS = 1e-6


def gated_sum(exp_table, expert_ids, slot_pos, gate_vals, residual):
    is_kept = slot_pos >= 0
    pick_rows = jax.vmap(lambda exp_rows, id_blk, pos_blk: exp_rows[id_blk, pos_blk])
    picked = pick_rows(exp_table, expert_ids, jnp.where(is_kept, slot_pos, 0))
    weight = jnp.where(is_kept, gate_vals, 0.0)
    mixed_sum = residual.astype(jnp.float32) + jnp.sum(weight[..., None] * picked.astype(jnp.float32), axis=3)
    return mixed_sum.astype(jnp.bfloat16)


def attention_block(combined, norm_w, w_query, w_key, w_value, w_out):
    y_wide = combined.astype(jnp.float32)
    inv_rms = lax.rsqrt(jnp.mean(y_wide * y_wide, axis=-1, keepdims=True) + NORM_EPS)
    x_in = (y_wide * inv_rms * norm_w).astype(jnp.bfloat16)
    q_heads = jnp.einsum('bld,dhe->blhe', x_in, w_query, preferred_element_type=jnp.float32).astype(jnp.bfloat16)
    k_heads = jnp.einsum('bld,dhe->blhe', x_in, w_key, preferred_element_type=jnp.float32).astype(jnp.bfloat16)
    v_heads = jnp.einsum('bld,dhe->blhe', x_in, w_value, preferred_element_type=jnp.float32).astype(jnp.bfloat16)
    head_dim = w_query.shape[2]
    seq_len = combined.shape[1]
    scores = jnp.einsum('bqhe,bkhe->bhqk', q_heads, k_heads, preferred_element_type=jnp.float32) * (head_dim ** -0.5)
    causal = jnp.arange(seq_len)[:, None] >= jnp.arange(seq_len)[None, :]
    attn_probs = jax.nn.softmax(jnp.where(causal, scores, -jnp.inf), axis=-1).astype(jnp.bfloat16)
    attn_out = jnp.einsum('bhqk,bkhe->bqhe', attn_probs, v_heads, preferred_element_type=jnp.float32).astype(jnp.bfloat16)
    out_proj = jnp.einsum('crif,ife->cre', attn_out, w_out, preferred_element_type=jnp.float32).astype(jnp.bfloat16)
    return (y_wide + out_proj.astype(jnp.float32)).astype(jnp.bfloat16)


def solution(mesh):
    stages = mesh.shape['pp']
    group_size = mesh.shape['ep']
    send_next = [(src_row, (src_row + 1) % stages) for src_row in range(stages)]
    tok_spec = P('pp', 'ep', None, None)
    wt_spec = P('pp', None, None, None)

    def device_step(expert_out, expert_ids, slot_ids, gate_vals, residual, norm_w, w_query, w_key, w_value, w_out):
        num_micro, seqs_dev, seq_len, d_model = residual.shape
        src_slots = expert_out.shape[2] // group_size
        returned = lax.all_to_all(expert_out, 'ep', 2, 1, tiled=True)
        block_base = lax.axis_index('ep') * src_slots
        slot_pos = jnp.where(slot_ids >= 0, slot_ids - block_base, -1)
        combined = gated_sum(returned, expert_ids, slot_pos, gate_vals, residual)
        arrived = lax.ppermute(combined, 'pp', send_next)
        flat_in = arrived.reshape(num_micro * seqs_dev, seq_len, d_model)
        result = attention_block(flat_in, norm_w[0], w_query[0], w_key[0], w_value[0], w_out[0])
        return result.reshape(num_micro, seqs_dev, seq_len, d_model)

    return jax.shard_map(device_step, mesh=mesh, in_specs=(tok_spec, tok_spec, tok_spec, tok_spec, tok_spec, P('pp', None), wt_spec, wt_spec, wt_spec, wt_spec), out_specs=tok_spec, check_vma=False)
```

profile of v0, /device:TPU:4, one launch (start us, length us, event | category | flops | bytes accessed | tf_op | source)
XLA Modules:
  0.0 2194.1 jit_solution(4853842765720781337)
XLA Ops:
  0.0 57.9 %copy.71 = bf16[6,4,320,4096]{3,0,1,2:T(8,128)(2,1)} copy(bf16[6,4,320,4096]{3,2,1,0:T(8,128)(2,1)} %param.10) | data formatting | bytes 125829120 | tf_op args[0]
  57.9 0.0 copy-start.4
  57.9 0.0 copy-start.2
  57.9 30.7 %all-to-all-start = ((bf16[6,4,320,4096]{3,0,1,2:T(8,128)(2,1)}), bf16[6,4,320,4096]{3,0,1,2:T(8,128)(2,1)}, u32[]{:S(2)}, u32[]{:S(2)}) async-start(bf16[6,4,320,4096]{3,0,1,2:T(8,128)(2,1)} %copy.71), calls=%async_computation | async-start | bytes 167772160 | tf_op jit(solution)/shard_map/all_to_all | solution.py:45
  88.6 0.0 copy-done.4
  88.7 0.0 copy-done.2
  88.8 0.1 fusion.52
  88.8 0.5 copy.80
  89.3 0.8 reshape.40
  90.1 60.0 %all-to-all-done = bf16[6,4,320,4096]{3,0,1,2:T(8,128)(2,1)} async-done(((bf16[6,4,320,4096]{3,0,1,2:T(8,128)(2,1)}), bf16[6,4,320,4096]{3,0,1,2:T(8,128)(2,1)}, u32[]{:S(2)}, u32[]{:S(2)}) %all-to-all-start) | async-done | bytes 62914592 | tf_op jit(solution)/shard_map/all_to_all | solution.py:45
  150.1 53.0 %copy.72 = bf16[6,4,2,160,4096]{4,3,1,2,0:T(8,128)(2,1)} copy(bf16[6,4,2,160,4096]{4,0,1,3,2:T(8,128)(2,1)} %bitcast.6) | data formatting | bytes 125829120 | tf_op jit(solution)/shard_map/all_to_all | solution.py:45
  203.1 295.9 %gather_fusion = bf16[6144,4096]{1,0:T(8,128)(2,1)} fusion(bf16[6,8,160,4096]{3,2,1,0:T(8,128)(2,1)} %bitcast.141, s32[6144]{0:T(1024)S(1)} %reshape.40), kind=kCustom, calls=%fused_computation | custom fusion | bytes 100737024 | tf_op jit(solution)/shard_map/vmap()/gather | solution.py:11
  499.0 0.0 copy-start.3
  499.1 0.0 copy-start.5
  499.1 101.9 %reshape.46 = f32[6,1,512,2,4096]{4,3,2,0,1:T(2,128)} reshape(bf16[6144,4096]{1,0:T(8,128)(2,1)} %gather_fusion) | data formatting | bytes 150994944 | tf_op jit(solution)/shard_map/convert_element_type | solution.py:14
  601.0 0.0 copy-done.3
  601.0 0.0 copy-done.5
  601.0 0.5 copy.70
  601.5 155.0 %multiply_reduce_fusion = f32[6,512,4096]{2,1,0:T(8,128)} fusion(f32[6,1,512,2,4096]{4,3,2,0,1:T(2,128)} %reshape.46, f32[6,512,2]{2,1,0:T(8,128)S(1)} %copy.70), kind=kLoop, calls=%fused_computation.8 | loop fusion | flops 37748736 | bytes 151019520 | tf_op jit(solution)/shard_map/reduce_sum | solution.py:14
  756.6 0.0 copy-start.8
  756.6 32.3 %fusion.12 = bf16[6,1,512,4096]{3,2,0,1:T(8,128)(2,1)} fusion(f32[6,512,4096]{2,1,0:T(8,128)} %multiply_reduce_fusion, bf16[6,1,512,4096]{3,2,1,0:T(8,128)(2,1)} %param.14), kind=kLoop, calls=%fused_computation.21 | loop fusion | flops 37748736 | bytes 100663296 | tf_op jit(solution)/shard_map/convert_element_type | solution.py:15
  788.9 0.0 collective-permute-start
  788.9 0.8 iota_compare_fusion
  789.6 575.3 %collective-permute-done = bf16[6,1,512,4096]{3,2,0,1:T(8,128)(2,1)S(1)} collective-permute-done((bf16[6,1,512,4096]{3,2,0,1:T(8,128)(2,1)}, bf16[6,1,512,4096]{3,2,0,1:T(8,128)(2,1)S(1)}, u32[]{:S(2)}, u32[]{:S(2)}) %collective-permute-start) | collective-permute-done | bytes 25165856 | tf_op jit(solution)/shard_map/ppermute | solution.py:49
  1365.0 0.0 copy-start
  1365.0 8.9 copy-done
  1373.9 5.9 fusion.8
  1379.8 0.0 copy-start.6
  1379.9 0.0 copy-done.8
  1379.9 113.8 %fusion.81 = bf16[6,512,32,128]{3,1,2,0:T(8,128)(2,1)} fusion(bf16[4096,32,128]{2,1,0:T(8,128)(2,1)} %bitcast.142, bf16[6,1,512,4096]{3,2,0,1:T(8,128)(2,1)} %copy-done, f32[4096]{0:T(1024)S(1)} %bitcast.145, f32[6,512]{1,0:T(8,128)S(1)} %add_rsqrt_fusion), kind=kOutput, calls=%fused_computation.38.clone.1 | convolution fusion | flops 103142129664 | bytes 83914752 | tf_op jit(solution)/shard_map/bld,dhe->blhe/dot_general | solution.py:23
  1493.7 0.0 copy-done.6
  1493.7 114.2 %fusion.17 = bf16[6,512,32,128]{3,1,2,0:T(8,128)(2,1)} fusion(bf16[4096,32,128]{2,1,0:T(8,128)(2,1)} %bitcast.143, bf16[6,1,512,4096]{3,2,0,1:T(8,128)(2,1)} %copy-done, f32[4096]{0:T(1024)S(1)} %bitcast.146, f32[6,512]{1,0:T(8,128)S(1)} %add_rsqrt_fusion), kind=kOutput, calls=%fused_computation.26 | convolution fusion | flops 103129546752 | bytes 83914752 | tf_op jit(solution)/shard_map/bld,dhe->blhe/dot_general | solution.py:22
  1607.9 0.0 copy-start.1
  1607.9 81.9 %fusion.28 = f32[6,32,512,512]{2,3,1,0:T(8,128)} fusion(bf16[6,512,32,128]{3,1,2,0:T(8,128)(2,1)} %fusion.17, bf16[6,512,32,128]{3,1,2,0:T(8,128)(2,1)} %fusion.81), kind=kOutput, calls=%fused_computation.37 | convolution fusion | flops 12884901888 | bytes 251658240 | tf_op jit(solution)/shard_map/bqhe,bkhe->bhqk/dot_general | solution.py:27
  1689.8 0.0 copy-done.1
  1689.8 0.0 copy-start.7
  1689.9 0.0 copy-start.9
  1689.9 192.4 %fusion.58 = (f32[6,32,512]{2,1,0:T(8,128)}, f32[6,32,512,512]{2,3,1,0:T(8,128)}) fusion(f32[6,32,512,512]{2,3,1,0:T(8,128)} %fusion.28, pred[512,512]{0,1:T(8,128)(4,1)S(1)} %copy-done.1), kind=kOutput, calls=%fused_computation.64 | output fusion | flops 301990400 | bytes 403308544 | tf_op jit(solution)/shard_map/sub | solution.py:29
  1882.2 0.0 copy-done.7
  1882.2 0.0 copy-done.9
  1882.2 0.0 copy-start.10
  1882.2 113.7 %fusion.19 = bf16[6,512,32,128]{3,1,2,0:T(8,128)(2,1)} fusion(bf16[4096,32,128]{2,1,0:T(8,128)(2,1)} %bitcast.144, bf16[6,1,512,4096]{3,2,0,1:T(8,128)(2,1)} %copy-done, f32[4096]{0:T(1024)S(1)} %bitcast.147, f32[6,512]{1,0:T(8,128)S(1)} %copy-done.7), kind=kOutput, calls=%fused_computation.28 | convolution fusion | flops 103129546752 | bytes 83914752 | tf_op jit(solution)/shard_map/bld,dhe->blhe/dot_general | solution.py:24
  1995.9 0.0 copy-done.10
  1995.9 79.1 %fusion.77 = bf16[6,512,32,128]{1,3,2,0:T(8,128)(2,1)} fusion(f32[6,32,512,512]{2,3,1,0:T(8,128)} %get-tuple-element.6, f32[6,32,512]{2,1,0:T(8,128)S(1)} %copy-done.10, bf16[6,512,32,128]{3,1,2,0:T(8,128)(2,1)} %fusion.19), kind=kOutput, calls=%fused_computation.35.clone.clone.clone.1 | convolution fusion | flops 12998148096 | bytes 252051456 | tf_op jit(solution)/shard_map/bhqk,bkhe->bqhe/dot_general | solution.py:30
  2075.0 118.7 %fusion.25 = bf16[6,1,512,4096]{3,2,1,0:T(8,128)(2,1)} fusion(bf16[6,1,512,4096]{3,2,0,1:T(8,128)(2,1)} %copy-done, bf16[1,32,128,4096]{3,2,1,0:T(8,128)(2,1)} %param.19, bf16[6,512,32,128]{1,3,2,0:T(8,128)(2,1)} %fusion.77), kind=kOutput, calls=%fused_computation.34 | convolution fusion | flops 103142129664 | bytes 109051904 | tf_op jit(solution)/shard_map/crif,ife->cre/dot_general | solution.py:31
  (6 shorter events, 0.1 us)
Async XLA Ops:
  57.9 30.8 %copy-start.4 = (s32[6,1,512,2]{2,3,1,0:T(2,128)S(1)}, s32[6,1,512,2]{2,3,1,0:T(2,128)}, u32[]{:S(2)}) copy-start(s32[6,1,512,2]{2,3,1,0:T(2,128)} %param.11) | copy-start | bytes 73732
  57.9 30.8 %copy-start.2 = (s32[6,1,512,2]{2,3,1,0:T(2,128)S(1)}, s32[6,1,512,2]{2,3,1,0:T(2,128)}, u32[]{:S(2)}) copy-start(s32[6,1,512,2]{2,3,1,0:T(2,128)} %param.12) | copy-start | bytes 73732
  57.9 92.2 %all-to-all-start = ((bf16[6,4,320,4096]{3,0,1,2:T(8,128)(2,1)}), bf16[6,4,320,4096]{3,0,1,2:T(8,128)(2,1)}, u32[]{:S(2)}, u32[]{:S(2)}) async-start(bf16[6,4,320,4096]{3,0,1,2:T(8,128)(2,1)} %copy.71), calls=%async_computation | async-start | bytes 167772160 | tf_op jit(solution)/shard_map/all_to_all | solution.py:45
  499.0 101.9 %copy-start.3 = (s32[6,1,512,2]{2,3,1,0:T(2,128)S(1)}, s32[6,1,512,2]{2,3,1,0:T(2,128)}, u32[]{:S(2)}) copy-start(s32[6,1,512,2]{2,3,1,0:T(2,128)} %param.12) | copy-start | bytes 73732
  499.1 101.9 %copy-start.5 = (f32[6,1,512,2]{2,3,1,0:T(2,128)S(1)}, f32[6,1,512,2]{2,3,1,0:T(2,128)}, u32[]{:S(2)}) copy-start(f32[6,1,512,2]{2,3,1,0:T(2,128)} %param.13) | copy-start | bytes 73732
  756.6 623.3 %copy-start.8 = (f32[1,4096]{1,0:T(1,128)S(1)}, f32[1,4096]{1,0:T(1,128)}, u32[]{:S(2)}) copy-start(f32[1,4096]{1,0:T(1,128)} %param.15) | copy-start | bytes 49156
  788.9 576.1 %collective-permute-start = (bf16[6,1,512,4096]{3,2,0,1:T(8,128)(2,1)}, bf16[6,1,512,4096]{3,2,0,1:T(8,128)(2,1)S(1)}, u32[]{:S(2)}, u32[]{:S(2)}) collective-permute-start(bf16[6,1,512,4096]{3,2,0,1:T(8,128)(2,1)} %fusion.12), channel_id=1, source_target_pairs={{0,2},{2,4},{4,6},{6,0},{1,3},{3,5},{5,7},{7,1}} | collective-permute-start | bytes 75497480 | tf_op jit(solution)/shard_map/ppermute | solution.py:49
  1365.0 8.9 copy-start
  1379.8 113.9 %copy-start.6 = (f32[6,512]{1,0:T(8,128)}, f32[6,512]{1,0:T(8,128)S(1)}, u32[]{:S(2)}) copy-start(f32[6,512]{1,0:T(8,128)S(1)} %add_rsqrt_fusion) | copy-start | bytes 36868
  1607.9 81.9 %copy-start.1 = (pred[512,512]{0,1:T(8,128)(4,1)S(1)}, pred[512,512]{0,1:T(8,128)(4,1)}, u32[]{:S(2)}) copy-start(pred[512,512]{0,1:T(8,128)(4,1)} %iota_compare_fusion) | copy-start | bytes 786436
  1689.8 192.4 %copy-start.7 = (f32[6,512]{1,0:T(8,128)S(1)}, f32[6,512]{1,0:T(8,128)}, u32[]{:S(2)}) copy-start(f32[6,512]{1,0:T(8,128)} %copy-done.6) | copy-start | bytes 36868
  1689.9 192.4 %copy-start.9 = (f32[1,4096]{1,0:T(1,128)S(1)}, f32[1,4096]{1,0:T(1,128)}, u32[]{:S(2)}) copy-start(f32[1,4096]{1,0:T(1,128)} %param.15) | copy-start | bytes 49156
  1882.2 113.7 %copy-start.10 = (f32[6,32,512]{2,1,0:T(8,128)S(1)}, f32[6,32,512]{2,1,0:T(8,128)}, u32[]{:S(2)}) copy-start(f32[6,32,512]{2,1,0:T(8,128)} %get-tuple-element.5) | copy-start | bytes 1179652
where the time goes:
time: 2210 us; the launch traced here: 2190 us
  waiting for transfers between devices  635 us (29%)
  matrix products  621 us (28%)
  local copies, waits for them, and re-layouts  520 us (24%)
  other arithmetic  387 us (18%)
  starting transfers between devices  30.7 us (1%)
    ppermute x1, waiting for transfers between devices, device_step(): arrived = lax.ppermute(combined, 'pp', send_next)  575 us
    gather x3, local copies, waits for them, and re-layouts, gated_sum(): exp_rows[id_blk, pos_blk]  297 us
    sub x1, other arithmetic, attention_block(): jax.nn.softmax(jnp.where(causal, scores, -jnp.inf), axis=-1)  192 us
    reduce_sum x1, other arithmetic, gated_sum(): jnp.sum(weight[..., None] * picked.astype(jnp.float32), axis=3)  155 us
    dot_general x1, matrix products, attention_block(): jnp.einsum('crif,ife->cre', attn_out, w_out, preferred_element_type=jnp.f...  119 us
    dot_general x1, matrix products, attention_block(): jnp.einsum('bld,dhe->blhe', x_in, w_query, preferred_element_type=jnp.flo...  114 us
    dot_general x1, matrix products, attention_block(): jnp.einsum('bld,dhe->blhe', x_in, w_key, preferred_element_type=jnp.float32)  114 us
    dot_general x1, matrix products, attention_block(): jnp.einsum('bld,dhe->blhe', x_in, w_value, preferred_element_type=jnp.flo...  114 us
  transfers between devices with their start and end apart: 2, of which 2 were waited for; matrix products, arithmetic and copies ran while one was open for 0% of the time, Pallas kernels for 0%

commit v1 on v0

v1 whole, which is shorter than its diff:
```python
import functools

import jax
import jax.numpy as jnp
from jax import lax
from jax.experimental import pallas as pl
from jax.experimental.pallas import tpu as pltpu
from jax.sharding import PartitionSpec as P


NORM_EPS = 1e-6
LOG2E = 1.4426950408889634
LANES = 128


def combine_kernel(micros, key_ref, gate_ref, expert_ref, res_ref, *refs):
    count = len(micros)
    out_refs = refs[:count]
    table_ref, pick_ref, wide_ref, own_sem, send_sem, recv_sem = refs[count:]
    tiles = table_ref.shape[0] // count
    experts, src_slots, width = table_ref.shape[1] // 2, table_ref.shape[2], table_ref.shape[3]
    num_rows, depth = pick_ref.shape
    tokens = num_rows // 2
    step, tile = pl.program_id(0), pl.program_id(1)
    slot = step * tiles + tile
    me = lax.axis_index('ep')
    mate = 1 - me

    def own_rows(step, tile, slot):
        cols = pl.ds(pl.multiple_of(tile * width, width), width)
        rows = pl.ds(pl.multiple_of(me * src_slots, src_slots), src_slots)
        return pltpu.make_async_copy(expert_ref.at[micros[0] + step, :, rows, cols], table_ref.at[slot, :experts], own_sem.at[slot])

    def mate_rows(step, tile, slot):
        cols = pl.ds(pl.multiple_of(tile * width, width), width)
        rows = pl.ds(pl.multiple_of(mate * src_slots, src_slots), src_slots)
        return pltpu.make_async_remote_copy(
            src_ref=expert_ref.at[micros[0] + step, :, rows, cols],
            dst_ref=table_ref.at[slot, experts:],
            send_sem=send_sem.at[slot],
            recv_sem=recv_sem.at[slot],
            device_id={'ep': mate},
            device_id_type=pl.DeviceIdType.MESH,
        )

    @pl.when(slot == 0)
    def _():
        barrier = pltpu.get_barrier_semaphore()
        pl.semaphore_signal(barrier, inc=1, device_id={'ep': mate}, device_id_type=pl.DeviceIdType.MESH)
        for at in range(min(2, tiles * count)):
            own_rows(at // tiles, at % tiles, at).start()
        pl.semaphore_wait(barrier, 1)

        def launch(at, carry):
            mate_rows(at // tiles, at % tiles, at).start()

            @pl.when(at >= 2)
            def _():
                own_rows(at // tiles, at % tiles, at).start()

            return carry

        lax.fori_loop(0, tiles * count, launch, 0)

    @pl.when(tile == 0)
    def _():
        for choice in range(2):
            rows = slice(choice * tokens, (choice + 1) * tokens)
            wide_ref[rows] = jnp.broadcast_to(gate_ref[0, choice:choice + 1, :], (LANES, tokens)).T
            keys = jnp.broadcast_to(key_ref[0, choice:choice + 1, :], (LANES, tokens)).T
            lane = lax.broadcasted_iota(jnp.int32, keys.shape, 1)
            for col in range(0, depth, LANES):
                pick_ref[rows, col:col + LANES] = jnp.where(keys == lane + col, 1.0, 0.0).astype(pick_ref.dtype)

    own_rows(step, tile, slot).wait()
    arriving = mate_rows(step, tile, slot)
    arriving.wait_recv()
    table = table_ref[slot].reshape(depth, width)
    picked = jnp.dot(pick_ref[...], table, preferred_element_type=jnp.float32)
    first, second = wide_ref[:tokens], wide_ref[tokens:]
    mixed = []
    for col in range(0, width, LANES):
        cols = slice(col, col + LANES)
        gated = first * picked[:tokens, cols] + second * picked[tokens:, cols]
        mixed.append((res_ref[0, 0, :, cols].astype(jnp.float32) + gated).astype(jnp.bfloat16))
    mixed = jnp.concatenate(mixed, axis=1)
    for at, out_ref in enumerate(out_refs):
        @pl.when(step == at)
        def _(out_ref=out_ref):
            out_ref[...] = mixed
    arriving.wait_send()


def combine(micros, call_id, keys, gates, expert_out, residual, width):
    _, experts, capacity, d_model = expert_out.shape
    src_slots = capacity // 2
    tokens = residual.shape[2]
    depth = 2 * experts * src_slots
    count, tiles, base = len(micros), d_model // width, micros[0]

    def out_spec(at):
        return pl.BlockSpec((tokens, width), lambda m, n: (0, jnp.where(m < at, 0, jnp.where(m > at, tiles - 1, n))))

    return pl.pallas_call(
        functools.partial(combine_kernel, micros),
        out_shape=[jax.ShapeDtypeStruct((tokens, d_model), jnp.bfloat16)] * count,
        grid=(count, tiles),
        in_specs=[
            pl.BlockSpec((1, 2, tokens), lambda m, n: (base + m, 0, 0)),
            pl.BlockSpec((1, 2, tokens), lambda m, n: (base + m, 0, 0)),
            pl.BlockSpec(memory_space=pl.ANY),
            pl.BlockSpec((1, 1, tokens, width), lambda m, n: (base + m, 0, 0, n)),
        ],
        out_specs=[out_spec(at) for at in range(count)],
        scratch_shapes=[
            pltpu.VMEM((count * tiles, 2 * experts, src_slots, width), jnp.bfloat16),
            pltpu.VMEM((2 * tokens, depth), jnp.bfloat16),
            pltpu.VMEM((2 * tokens, LANES), jnp.float32),
            pltpu.SemaphoreType.DMA((count * tiles,)),
            pltpu.SemaphoreType.DMA((count * tiles,)),
            pltpu.SemaphoreType.DMA((count * tiles,)),
        ],
        compiler_params=pltpu.CompilerParams(vmem_limit_bytes=60 << 20, collective_id=call_id, has_side_effects=True),
        cost_estimate=pl.CostEstimate(flops=4 * count * tokens * depth * d_model, bytes_accessed=2 * count * d_model * (depth + 2 * tokens), transcendentals=0),
        name='combine',
    )(keys, gates, expert_out, residual)


def regroup_kernel(wt_ref, out_ref, wide_ref):
    rows, heads, head_dim = wt_ref.shape[1:]
    wide_ref[...] = wt_ref[0].astype(jnp.float32).reshape(rows * heads, head_dim)
    for head in range(heads):
        out_ref[:, head * head_dim:(head + 1) * head_dim] = wide_ref[pl.ds(head, rows, stride=heads), :].astype(out_ref.dtype)


def regroup(weight, rows, heads):
    _, d_model, num_heads, head_dim = weight.shape
    return pl.pallas_call(
        regroup_kernel,
        out_shape=jax.ShapeDtypeStruct((d_model, num_heads * head_dim), weight.dtype),
        grid=(d_model // rows, num_heads // heads),
        in_specs=[pl.BlockSpec((1, rows, heads, head_dim), lambda r, h: (0, r, h, 0))],
        out_specs=pl.BlockSpec((rows, heads * head_dim), lambda r, h: (r, h)),
        scratch_shapes=[pltpu.VMEM((rows * heads, head_dim), jnp.float32)],
        compiler_params=pltpu.CompilerParams(vmem_limit_bytes=32 << 20),
        cost_estimate=pl.CostEstimate(flops=10 ** 10, bytes_accessed=4 * d_model * num_heads * head_dim, transcendentals=0),
        name='regroup',
    )(weight)


def attention_kernel(y_ref, norm_ref, wq_ref, wk_ref, wv_ref, out_ref, x_ref, q_ref, k_ref, v_ref):
    seq_len, _ = y_ref.shape
    head_dim = LANES
    block = seq_len // 2

    @pl.when(pl.program_id(0) == 0)
    def _():
        strip = 32

        def norm_strip(step, carry):
            rows = pl.ds(pl.multiple_of(step * strip, strip), strip)
            y_wide = y_ref[rows, :].astype(jnp.float32)
            inv_rms = lax.rsqrt(jnp.mean(y_wide * y_wide, axis=-1, keepdims=True) + NORM_EPS)
            x_ref[rows, :] = (y_wide * inv_rms * norm_ref[...]).astype(x_ref.dtype)
            return carry

        lax.fori_loop(0, seq_len // strip, norm_strip, 0)

    for wt_ref, dst_ref in ((wq_ref, q_ref), (wk_ref, k_ref), (wv_ref, v_ref)):
        dst_ref[...] = jnp.dot(x_ref[...], wt_ref[...], preferred_element_type=jnp.float32).astype(dst_ref.dtype)

    factor = (head_dim ** -0.5) * LOG2E
    row_pos = lax.broadcasted_iota(jnp.int32, (block, block), 0)
    col_pos = lax.broadcasted_iota(jnp.int32, (block, block), 1)
    seen = row_pos >= col_pos
    contract = (((1,), (1,)), ((), ()))
    for head in range(out_ref.shape[1] // head_dim):
        cols = slice(head * head_dim, (head + 1) * head_dim)
        for part in range(2):
            rows = slice(part * block, (part + 1) * block)
            query = q_ref[rows, cols]
            pieces = []
            if part:
                pieces.append(lax.dot_general(query, k_ref[:block, cols], contract, preferred_element_type=jnp.float32))
            last = lax.dot_general(query, k_ref[rows, cols], contract, preferred_element_type=jnp.float32)
            pieces.append(jnp.where(seen, last, -jnp.inf))
            scores = jnp.concatenate(pieces, axis=1) if part else pieces[0]
            top = jnp.max(scores, axis=1, keepdims=True)
            grown = jnp.exp2((scores - top) * factor)
            probs = (grown * (1.0 / jnp.sum(grown, axis=1, keepdims=True))).astype(jnp.bfloat16)
            mixed = jnp.dot(probs, v_ref[:(part + 1) * block, cols], preferred_element_type=jnp.float32)
            out_ref[rows, cols] = mixed.astype(out_ref.dtype)


def attention(arrived, norm_w, weights, width):
    seq_len, d_model = arrived.shape
    depth = weights[0].shape[1]
    wt_spec = pl.BlockSpec((d_model, width), lambda h: (0, h))
    head_scratch = pltpu.VMEM((seq_len, width), jnp.bfloat16)
    return pl.pallas_call(
        attention_kernel,
        out_shape=jax.ShapeDtypeStruct((seq_len, depth), jnp.bfloat16),
        grid=(depth // width,),
        in_specs=[
            pl.BlockSpec((seq_len, d_model), lambda h: (0, 0)),
            pl.BlockSpec((1, d_model), lambda h: (0, 0)),
            wt_spec, wt_spec, wt_spec,
        ],
        out_specs=pl.BlockSpec((seq_len, width), lambda h: (0, h)),
        scratch_shapes=[pltpu.VMEM((seq_len, d_model), jnp.bfloat16), head_scratch, head_scratch, head_scratch],
        compiler_params=pltpu.CompilerParams(vmem_limit_bytes=60 << 20),
        cost_estimate=pl.CostEstimate(flops=6 * seq_len * d_model * depth, bytes_accessed=6 * d_model * depth, transcendentals=0),
        name='attention',
    )(arrived, norm_w, *weights)


def project_kernel(attn_ref, wt_ref, res_ref, *refs):
    out_ref = refs[-1]
    proj = jnp.dot(attn_ref[...], wt_ref[...], preferred_element_type=jnp.float32).astype(jnp.bfloat16)
    out_ref[0, 0] = (res_ref[...].astype(jnp.float32) + proj.astype(jnp.float32)).astype(out_ref.dtype)


def project(micro, attn_out, w_out, arrived, result, out_shape, tile):
    tokens, depth = attn_out.shape
    d_model = w_out.shape[1]
    in_specs = [
        pl.BlockSpec((tokens, depth), lambda n: (0, 0)),
        pl.BlockSpec((depth, tile), lambda n: (0, n)),
        pl.BlockSpec((tokens, tile), lambda n: (0, n)),
    ]
    operands = [attn_out, w_out, arrived]
    aliases = {}
    if result is not None:
        in_specs.append(pl.BlockSpec(memory_space=pl.ANY))
        operands.append(result)
        aliases = {3: 0}
    return pl.pallas_call(
        project_kernel,
        out_shape=jax.ShapeDtypeStruct(out_shape, jnp.bfloat16),
        grid=(d_model // tile,),
        in_specs=in_specs,
        out_specs=pl.BlockSpec((1, 1, tokens, tile), lambda n: (micro, 0, 0, n)),
        input_output_aliases=aliases,
        compiler_params=pltpu.CompilerParams(vmem_limit_bytes=60 << 20),
        cost_estimate=pl.CostEstimate(flops=2 * tokens * depth * d_model, bytes_accessed=2 * depth * d_model, transcendentals=0),
        name='project',
    )(*operands)


def solution(mesh):
    stages = mesh.shape['pp']
    group_size = mesh.shape['ep']
    send_next = [(src, (src + 1) % stages) for src in range(stages)]
    tok_spec = P('pp', 'ep', None, None)
    wt_spec = P('pp', None, None, None)

    def device_step(expert_out, expert_ids, slot_ids, gate_vals, residual, norm_w, w_query, w_key, w_value, w_out):
        num_micro, _, _, d_model = residual.shape
        experts, capacity = expert_out.shape[1:3]
        src_slots = capacity // group_size
        num_experts = experts * group_size
        position = lax.axis_index('ep').astype(jnp.int32)

        place = (expert_ids[:, 0] - position * experts) % num_experts
        keys = jnp.where(slot_ids[:, 0] >= 0, place * src_slots + slot_ids[:, 0] - position * src_slots, -1)
        keys = jnp.swapaxes(keys, 1, 2)
        gates = jnp.swapaxes(gate_vals[:, 0], 1, 2)

        arrived = []
        combined = []
        for call_id, micros in enumerate(((0,), (1, 2), (3, 4, 5))):
            if combined:
                keys = lax.optimization_barrier((keys, combined[-1]))[0]
            rows = combine(micros, call_id, keys, gates, expert_out, residual, 512)
            combined.extend(rows)
            for micro, row in zip(micros, rows):
                arrived.append(lax.ppermute(row, 'pp', send_next))
        raw = lax.optimization_barrier((w_query, w_key, w_value, combined[-1]))[:3]
        weights = [regroup(wt, 256, 8) for wt in raw]

        flat_out = w_out[0].reshape(-1, d_model)
        result = None
        for micro in range(num_micro):
            rows = arrived[micro]
            if micro:
                rows, result = lax.optimization_barrier((rows, result))
            attn_out = attention(rows, norm_w, weights, 512)
            result = project(micro, attn_out, flat_out, rows, result, residual.shape, 512)
        return result

    return jax.shard_map(device_step, mesh=mesh, in_specs=(tok_spec, tok_spec, tok_spec, tok_spec, tok_spec, P('pp', None), wt_spec, wt_spec, wt_spec, wt_spec), out_specs=tok_spec, check_vma=False)
```

time: 2210 us -> 956 us (0.43)
  Pallas kernels: 0 us -> 936 us
  waiting for transfers between devices: 635 us -> 0.02 us
  matrix products: 621 us -> 0 us
  local copies, waits for them, and re-layouts: 520 us -> 0 us
  other arithmetic: 387 us -> 1.42 us
  starting transfers between devices: 30.7 us -> 6.6 us
    pallas_call x0 -> x18, Pallas kernels: none -> 936 us  [the longest x6 542 us: attention(): pl.pallas_call(attention_kernel, out_shape=jax.ShapeDtypeStruct((seq_len,...]
    dot_general x6 -> x0, matrix products: 621 us -> none  [the longest x1 119 us: attention_block(): jnp.einsum('crif,ife->cre', attn_out, w_out, preferred_element_type=jnp.f...]
    ppermute x1 -> x6, waiting for transfers between devices: 575 us -> 0.02 us  [device_step(): arrived.append(lax.ppermute(row, 'pp', send_next))]
    gather x3 -> x0, local copies, waits for them, and re-layouts: 297 us -> none  [gated_sum(): exp_rows[id_blk, pos_blk]]
    sub x1 -> x0, other arithmetic: 192 us -> none  [attention_block(): jax.nn.softmax(jnp.where(causal, scores, -jnp.inf), axis=-1)]
    reduce_sum x2 -> x0, other arithmetic: 161 us -> none  [the longest x1 155 us: gated_sum(): jnp.sum(weight[..., None] * picked.astype(jnp.float32), axis=3)]
    convert_element_type x1 -> x0, local copies, waits for them, and re-layouts: 102 us -> none  [gated_sum(): picked.astype(jnp.float32)]
    unnamed x24 -> x0, local copies, waits for them, and re-layouts: 66.9 us -> none
  transfers between devices with their start and end apart: 2 -> 6, of which waited for: 2 -> 0; matrix products, arithmetic and copies ran while one was open for 0% -> 0% of each run, Pallas kernels for 0% -> 85%
where the time goes in v1:
time: 956 us; the launch traced here: 944 us
  Pallas kernels  936 us (98%)
    pallas_call x6, Pallas kernels, attention(): pl.pallas_call(attention_kernel, out_shape=jax.ShapeDtypeStruct((seq_len,...  542 us
    pallas_call x3, Pallas kernels, regroup(): pl.pallas_call(regroup_kernel, out_shape=jax.ShapeDtypeStruct((d_model, n...  154 us
    pallas_call x6, Pallas kernels, project(): pl.pallas_call(project_kernel, out_shape=jax.ShapeDtypeStruct(out_shape,...  142 us
    pallas_call x3, Pallas kernels, combine(): pl.pallas_call(functools.partial(combine_kernel, micros), out_shape=[jax....  98.4 us
  transfers between devices with their start and end apart: 6, of which 0 were waited for; matrix products, arithmetic and copies ran while one was open for 0% of the time, Pallas kernels for 85%

profile of v1, /device:TPU:4, one launch (start us, length us, event | category | flops | bytes accessed | tf_op | source)
XLA Modules:
  0.0 944.2 jit_solution(14035817336325881880)
XLA Ops:
  0.0 1.4 fusion.key_ref
  1.4 17.2 %combine.3 = bf16[512,4096]{1,0:T(8,128)(2,1)} custom-call(s32[6,2,512]{2,1,0:T(2,128)} %fusion.key_ref, f32[6,2,512]{2,1,0:T(2,128)} %bitcast.27, bf16[6,4,320,4096]{3,2,1,0:T(8,128)(2,1)} %expert_ref.5, bf16[6,1,512,4096]{3,2,1,0:T(8,128)(2,1)} %res_ref.5), custom_call_target="tpu_custom_call" | custom-call | flops 10737418240 | bytes 18874368 | tf_op jit(solution)/shard_map/combine/pallas_call | solution.py:104
  18.7 1.5 collective-permute-start.5
  20.2 32.8 %combine.4 = (bf16[512,4096]{1,0:T(8,128)(2,1)}, bf16[512,4096]{1,0:T(8,128)(2,1)}) custom-call(s32[6,2,512]{2,1,0:T(2,128)} %fusion.key_ref, f32[6,2,512]{2,1,0:T(2,128)} %bitcast.28, bf16[6,4,320,4096]{3,2,1,0:T(8,128)(2,1)} %expert_ref.5, bf16[6,1,512,4096]{3,2,1,0:T(8,128)(2,1)} %res_ref.5), custom_call_target="tpu_custom_call" | custom-call | flops 21474836480 | bytes 37748736 | tf_op jit(solution)/shard_map/combine/pallas_call | solution.py:104
  53.0 0.1 collective-permute-start.4
  53.1 1.9 collective-permute-start.3
  55.0 48.4 %combine.5 = (bf16[512,4096]{1,0:T(8,128)(2,1)}, bf16[512,4096]{1,0:T(8,128)(2,1)}, bf16[512,4096]{1,0:T(8,128)(2,1)}) custom-call(s32[6,2,512]{2,1,0:T(2,128)} %fusion.key_ref, f32[6,2,512]{2,1,0:T(2,128)} %bitcast.29, bf16[6,4,320,4096]{3,2,1,0:T(8,128)(2,1)} %expert_ref.5, bf16[6,1,512,4096]{3,2,1,0:T(8,128)(2,1)} %res_ref.5), custom_call_target="tpu_custom_call" | custom-call | flops 32212254720 | bytes 56623104 | tf_op jit(solution)/shard_map/combine/pallas_call | solution.py:104
  103.4 1.5 collective-permute-start.1
  104.9 1.5 collective-permute-start
  106.4 51.2 %regroup.3.wq_ref = bf16[4096,4096]{1,0:T(8,128)(2,1)} custom-call(bf16[1,4096,32,128]{3,2,1,0:T(8,128)(2,1)} %wt_ref), custom_call_target="tpu_custom_call" | custom-call | flops 10000000000 | bytes 67108864 | tf_op jit(solution)/shard_map/regroup/pallas_call | solution.py:138
  157.6 51.2 %regroup.4.wk_ref = bf16[4096,4096]{1,0:T(8,128)(2,1)} custom-call(bf16[1,4096,32,128]{3,2,1,0:T(8,128)(2,1)} %wt_ref.1), custom_call_target="tpu_custom_call" | custom-call | flops 10000000000 | bytes 67108864 | tf_op jit(solution)/shard_map/regroup/pallas_call | solution.py:138
  208.8 51.2 %regroup.5.wv_ref = bf16[4096,4096]{1,0:T(8,128)(2,1)} custom-call(bf16[1,4096,32,128]{3,2,1,0:T(8,128)(2,1)} %wt_ref.2), custom_call_target="tpu_custom_call" | custom-call | flops 10000000000 | bytes 67108864 | tf_op jit(solution)/shard_map/regroup/pallas_call | solution.py:138
  260.0 0.0 collective-permute-done.5.y_ref.res_ref
  260.0 0.1 collective-permute-start.2
  260.1 90.3 %attention.6.attn_ref = bf16[512,4096]{1,0:T(8,128)(2,1)} custom-call(bf16[512,4096]{1,0:T(8,128)(2,1)} %collective-permute-done.5.y_ref.res_ref, f32[1,4096]{1,0:T(1,128)} %norm_ref.11, bf16[4096,4096]{1,0:T(8,128)(2,1)} %regroup.3.wq_ref, bf16[4096,4096]{1,0:T(8,128)(2,1)} %regroup.4.wk_ref, bf16[4096,4096]{1,0:T(8,128)(2,1)} %regroup.5.wv_ref), custom_call_target="tpu_custom_call" | custom-call | flops 51539607552 | bytes 100663296 | tf_op jit(solution)/shard_map/attention/pallas_call | solution.py:200
  350.3 23.7 %project.6.refs_0_ = bf16[6,1,512,4096]{3,2,1,0:T(8,128)(2,1)} custom-call(bf16[512,4096]{1,0:T(8,128)(2,1)} %attention.6.attn_ref, bf16[4096,4096]{1,0:T(8,128)(2,1)} %bitcast.21, bf16[512,4096]{1,0:T(8,128)(2,1)} %collective-permute-done.5.y_ref.res_ref), custom_call_target="tpu_custom_call" | custom-call | flops 17179869184 | bytes 33554432 | tf_op jit(solution)/shard_map/project/pallas_call | solution.py:237
  374.0 0.0 collective-permute-done.4.y_ref.res_ref
  374.0 90.6 %attention.7.attn_ref = bf16[512,4096]{1,0:T(8,128)(2,1)} custom-call(bf16[512,4096]{1,0:T(8,128)(2,1)} %collective-permute-done.4.y_ref.res_ref, f32[1,4096]{1,0:T(1,128)} %norm_ref.11, bf16[4096,4096]{1,0:T(8,128)(2,1)} %regroup.3.wq_ref, bf16[4096,4096]{1,0:T(8,128)(2,1)} %regroup.4.wk_ref, bf16[4096,4096]{1,0:T(8,128)(2,1)} %regroup.5.wv_ref), custom_call_target="tpu_custom_call" | custom-call | flops 51539607552 | bytes 100663296 | tf_op jit(solution)/shard_map/attention/pallas_call | solution.py:200
  464.6 23.7 %project.7.refs_0_ = bf16[6,1,512,4096]{3,2,1,0:T(8,128)(2,1)} custom-call(bf16[512,4096]{1,0:T(8,128)(2,1)} %attention.7.attn_ref, bf16[4096,4096]{1,0:T(8,128)(2,1)} %bitcast.22, bf16[512,4096]{1,0:T(8,128)(2,1)} %collective-permute-done.4.y_ref.res_ref, bf16[6,1,512,4096]{3,2,1,0:T(8,128)(2,1)} %project.6.refs_0_), custom_call_target="tpu_custom_call", output_to_operand_aliasing={{}: (3, {})} | custom-call | flops 17179869184 | bytes 33554432 | tf_op jit(solution)/shard_map/project/pallas_call | solution.py:237
  488.3 0.0 collective-permute-done.3.y_ref.res_ref
  488.3 90.1 %attention.8.attn_ref = bf16[512,4096]{1,0:T(8,128)(2,1)} custom-call(bf16[512,4096]{1,0:T(8,128)(2,1)} %collective-permute-done.3.y_ref.res_ref, f32[1,4096]{1,0:T(1,128)} %norm_ref.11, bf16[4096,4096]{1,0:T(8,128)(2,1)} %regroup.3.wq_ref, bf16[4096,4096]{1,0:T(8,128)(2,1)} %regroup.4.wk_ref, bf16[4096,4096]{1,0:T(8,128)(2,1)} %regroup.5.wv_ref), custom_call_target="tpu_custom_call" | custom-call | flops 51539607552 | bytes 100663296 | tf_op jit(solution)/shard_map/attention/pallas_call | solution.py:200
  578.4 23.7 %project.8.refs_0_ = bf16[6,1,512,4096]{3,2,1,0:T(8,128)(2,1)} custom-call(bf16[512,4096]{1,0:T(8,128)(2,1)} %attention.8.attn_ref, bf16[4096,4096]{1,0:T(8,128)(2,1)} %bitcast.23, bf16[512,4096]{1,0:T(8,128)(2,1)} %collective-permute-done.3.y_ref.res_ref, bf16[6,1,512,4096]{3,2,1,0:T(8,128)(2,1)} %project.7.refs_0_), custom_call_target="tpu_custom_call", output_to_operand_aliasing={{}: (3, {})} | custom-call | flops 17179869184 | bytes 33554432 | tf_op jit(solution)/shard_map/project/pallas_call | solution.py:237
  602.1 0.0 collective-permute-done.2.y_ref.res_ref
  602.1 90.2 %attention.9.attn_ref = bf16[512,4096]{1,0:T(8,128)(2,1)} custom-call(bf16[512,4096]{1,0:T(8,128)(2,1)} %collective-permute-done.2.y_ref.res_ref, f32[1,4096]{1,0:T(1,128)} %norm_ref.11, bf16[4096,4096]{1,0:T(8,128)(2,1)} %regroup.3.wq_ref, bf16[4096,4096]{1,0:T(8,128)(2,1)} %regroup.4.wk_ref, bf16[4096,4096]{1,0:T(8,128)(2,1)} %regroup.5.wv_ref), custom_call_target="tpu_custom_call" | custom-call | flops 51539607552 | bytes 100663296 | tf_op jit(solution)/shard_map/attention/pallas_call | solution.py:200
  692.3 23.7 %project.9.refs_0_ = bf16[6,1,512,4096]{3,2,1,0:T(8,128)(2,1)} custom-call(bf16[512,4096]{1,0:T(8,128)(2,1)} %attention.9.attn_ref, bf16[4096,4096]{1,0:T(8,128)(2,1)} %bitcast.24, bf16[512,4096]{1,0:T(8,128)(2,1)} %collective-permute-done.2.y_ref.res_ref, bf16[6,1,512,4096]{3,2,1,0:T(8,128)(2,1)} %project.8.refs_0_), custom_call_target="tpu_custom_call", output_to_operand_aliasing={{}: (3, {})} | custom-call | flops 17179869184 | bytes 33554432 | tf_op jit(solution)/shard_map/project/pallas_call | solution.py:237
  716.0 0.0 collective-permute-done.1.y_ref.res_ref
  716.0 90.2 %attention.10.attn_ref = bf16[512,4096]{1,0:T(8,128)(2,1)} custom-call(bf16[512,4096]{1,0:T(8,128)(2,1)} %collective-permute-done.1.y_ref.res_ref, f32[1,4096]{1,0:T(1,128)} %norm_ref.11, bf16[4096,4096]{1,0:T(8,128)(2,1)} %regroup.3.wq_ref, bf16[4096,4096]{1,0:T(8,128)(2,1)} %regroup.4.wk_ref, bf16[4096,4096]{1,0:T(8,128)(2,1)} %regroup.5.wv_ref), custom_call_target="tpu_custom_call" | custom-call | flops 51539607552 | bytes 100663296 | tf_op jit(solution)/shard_map/attention/pallas_call | solution.py:200
  806.2 23.7 %project.10.refs_0_ = bf16[6,1,512,4096]{3,2,1,0:T(8,128)(2,1)} custom-call(bf16[512,4096]{1,0:T(8,128)(2,1)} %attention.10.attn_ref, bf16[4096,4096]{1,0:T(8,128)(2,1)} %bitcast.25, bf16[512,4096]{1,0:T(8,128)(2,1)} %collective-permute-done.1.y_ref.res_ref, bf16[6,1,512,4096]{3,2,1,0:T(8,128)(2,1)} %project.9.refs_0_), custom_call_target="tpu_custom_call", output_to_operand_aliasing={{}: (3, {})} | custom-call | flops 17179869184 | bytes 33554432 | tf_op jit(solution)/shard_map/project/pallas_call | solution.py:237
  829.9 0.0 collective-permute-done.y_ref.res_ref
  829.9 90.3 %attention.11.attn_ref = bf16[512,4096]{1,0:T(8,128)(2,1)} custom-call(bf16[512,4096]{1,0:T(8,128)(2,1)} %collective-permute-done.y_ref.res_ref, f32[1,4096]{1,0:T(1,128)} %norm_ref.11, bf16[4096,4096]{1,0:T(8,128)(2,1)} %regroup.3.wq_ref, bf16[4096,4096]{1,0:T(8,128)(2,1)} %regroup.4.wk_ref, bf16[4096,4096]{1,0:T(8,128)(2,1)} %regroup.5.wv_ref), custom_call_target="tpu_custom_call" | custom-call | flops 51539607552 | bytes 100663296 | tf_op jit(solution)/shard_map/attention/pallas_call | solution.py:200
  920.2 23.7 %project.11 = bf16[6,1,512,4096]{3,2,1,0:T(8,128)(2,1)} custom-call(bf16[512,4096]{1,0:T(8,128)(2,1)} %attention.11.attn_ref, bf16[4096,4096]{1,0:T(8,128)(2,1)} %bitcast.26, bf16[512,4096]{1,0:T(8,128)(2,1)} %collective-permute-done.y_ref.res_ref, bf16[6,1,512,4096]{3,2,1,0:T(8,128)(2,1)} %project.10.refs_0_), custom_call_target="tpu_custom_call", output_to_operand_aliasing={{}: (3, {})} | custom-call | flops 17179869184 | bytes 33554432 | tf_op jit(solution)/shard_map/project/pallas_call | solution.py:237
Async XLA Ops:
  18.7 241.3 %collective-permute-start.5 = (bf16[512,4096]{1,0:T(8,128)(2,1)}, bf16[512,4096]{1,0:T(8,128)(2,1)}, u32[]{:S(2)}, u32[]{:S(2)}) collective-permute-start(bf16[512,4096]{1,0:T(8,128)(2,1)} %combine.3), channel_id=1, source_target_pairs={{0,2},{2,4},{4,6},{6,0},{1,3},{3,5},{5,7},{7,1}} | collective-permute-start | bytes 12582920 | tf_op jit(solution)/shard_map/ppermute | solution.py:277
  53.0 321.0 %collective-permute-start.4 = (bf16[512,4096]{1,0:T(8,128)(2,1)}, bf16[512,4096]{1,0:T(8,128)(2,1)}, u32[]{:S(2)}, u32[]{:S(2)}) collective-permute-start(bf16[512,4096]{1,0:T(8,128)(2,1)} %get-tuple-element.31), channel_id=1, source_target_pairs={{0,2},{2,4},{4,6},{6,0},{1,3},{3,5},{5,7},{7,1}} | collective-permute-start | bytes 12582920 | tf_op jit(solution)/shard_map/ppermute | solution.py:277
  53.1 435.2 %collective-permute-start.3 = (bf16[512,4096]{1,0:T(8,128)(2,1)}, bf16[512,4096]{1,0:T(8,128)(2,1)}, u32[]{:S(2)}, u32[]{:S(2)}) collective-permute-start(bf16[512,4096]{1,0:T(8,128)(2,1)} %get-tuple-element.26), channel_id=1, source_target_pairs={{0,2},{2,4},{4,6},{6,0},{1,3},{3,5},{5,7},{7,1}} | collective-permute-start | bytes 12582920 | tf_op jit(solution)/shard_map/ppermute | solution.py:277
  103.4 612.6 %collective-permute-start.1 = (bf16[512,4096]{1,0:T(8,128)(2,1)}, bf16[512,4096]{1,0:T(8,128)(2,1)}, u32[]{:S(2)}, u32[]{:S(2)}) collective-permute-start(bf16[512,4096]{1,0:T(8,128)(2,1)} %get-tuple-element.29), channel_id=1, source_target_pairs={{0,2},{2,4},{4,6},{6,0},{1,3},{3,5},{5,7},{7,1}} | collective-permute-start | bytes 12582920 | tf_op jit(solution)/shard_map/ppermute | solution.py:277
  104.9 725.0 %collective-permute-start = (bf16[512,4096]{1,0:T(8,128)(2,1)}, bf16[512,4096]{1,0:T(8,128)(2,1)}, u32[]{:S(2)}, u32[]{:S(2)}) collective-permute-start(bf16[512,4096]{1,0:T(8,128)(2,1)} %get-tuple-element.28), channel_id=1, source_target_pairs={{0,2},{2,4},{4,6},{6,0},{1,3},{3,5},{5,7},{7,1}} | collective-permute-start | bytes 12582920 | tf_op jit(solution)/shard_map/ppermute | solution.py:277
  260.0 342.1 %collective-permute-start.2 = (bf16[512,4096]{1,0:T(8,128)(2,1)}, bf16[512,4096]{1,0:T(8,128)(2,1)}, u32[]{:S(2)}, u32[]{:S(2)}) collective-permute-start(bf16[512,4096]{1,0:T(8,128)(2,1)} %get-tuple-element.30), channel_id=1, source_target_pairs={{0,2},{2,4},{4,6},{6,0},{1,3},{3,5},{5,7},{7,1}} | collective-permute-start | bytes 12582920 | tf_op jit(solution)/shard_map/ppermute | solution.py:277

commit v2 on v1

--- a/solution.py
+++ b/solution.py
@@ -127,10 +127,17 @@
 
 
 def regroup_kernel(wt_ref, out_ref, wide_ref):
-    rows, heads, head_dim = wt_ref.shape[1:]
-    wide_ref[...] = wt_ref[0].astype(jnp.float32).reshape(rows * heads, head_dim)
-    for head in range(heads):
-        out_ref[:, head * head_dim:(head + 1) * head_dim] = wide_ref[pl.ds(head, rows, stride=heads), :].astype(out_ref.dtype)
+    heads, head_dim = wt_ref.shape[2:]
+    strip = wide_ref.shape[0] // heads
+
+    def regroup_strip(at, carry):
+        rows = pl.ds(pl.multiple_of(at * strip, strip), strip)
+        wide_ref[...] = wt_ref[0, rows].astype(jnp.float32).reshape(strip * heads, head_dim)
+        for head in range(heads):
+            out_ref[rows, head * head_dim:(head + 1) * head_dim] = wide_ref[pl.ds(head, strip, stride=heads), :].astype(out_ref.dtype)
+        return carry
+
+    lax.fori_loop(0, wt_ref.shape[1] // strip, regroup_strip, 0)
 
 
 def regroup(weight, rows, heads):
@@ -141,109 +148,153 @@
         grid=(d_model // rows, num_heads // heads),
         in_specs=[pl.BlockSpec((1, rows, heads, head_dim), lambda r, h: (0, r, h, 0))],
         out_specs=pl.BlockSpec((rows, heads * head_dim), lambda r, h: (r, h)),
-        scratch_shapes=[pltpu.VMEM((rows * heads, head_dim), jnp.float32)],
+        scratch_shapes=[pltpu.VMEM((128 * heads, head_dim), jnp.float32)],
         compiler_params=pltpu.CompilerParams(vmem_limit_bytes=32 << 20),
         cost_estimate=pl.CostEstimate(flops=10 ** 10, bytes_accessed=4 * d_model * num_heads * head_dim, transcendentals=0),
         name='regroup',
     )(weight)
 
 
-def attention_kernel(y_ref, norm_ref, wq_ref, wk_ref, wv_ref, out_ref, x_ref, q_ref, k_ref, v_ref):
-    seq_len, _ = y_ref.shape
-    head_dim = LANES
+def attend(q_ref, k_ref, v_ref, head, part):
+    seq_len, head_dim = q_ref.shape[0], LANES
     block = seq_len // 2
-
-    @pl.when(pl.program_id(0) == 0)
-    def _():
+    cols = slice(head * head_dim, (head + 1) * head_dim)
+    rows = slice(part * block, (part + 1) * block)
+    contract = (((1,), (1,)), ((), ()))
+    query = q_ref[rows, cols]
+    seen = lax.broadcasted_iota(jnp.int32, (block, block), 0) >= lax.broadcasted_iota(jnp.int32, (block, block), 1)
+    last = lax.dot_general(query, k_ref[rows, cols], contract, preferred_element_type=jnp.float32)
+    scores = jnp.where(seen, last, -jnp.inf)
+    if part:
+        early = lax.dot_general(query, k_ref[:block, cols], contract, preferred_element_type=jnp.float32)
+        scores = jnp.concatenate([early, scores], axis=1)
+    top = jnp.max(scores, axis=1, keepdims=True)
+    grown = jnp.exp2((scores - top) * ((head_dim ** -0.5) * LOG2E))
+    probs = (grown * (1.0 / jnp.sum(grown, axis=1, keepdims=True))).astype(jnp.bfloat16)
+    mixed = jnp.dot(probs, v_ref[:(part + 1) * block, cols], preferred_element_type=jnp.float32)
+    return rows, mixed.astype(jnp.bfloat16)
+
+
+def attention_kernel(norm_ref, y_hbm, wq_hbm, wk_hbm, wv_hbm, wo_hbm, *refs):
+    (out_ref, y_ref, x_ref, attn_ref, wt_ref, wo_ref, qa_ref, ka_ref, va_ref, qb_ref, kb_ref, vb_ref, y_sem, wt_sem, wo_sem) = refs[-15:]
+    seq_len, d_model = y_ref.shape
+    width = wt_ref.shape[3]
+    pair = width // 2
+    steps = wq_hbm.shape[1] // width
+    tile = wo_ref.shape[2]
+    step = pl.program_id(0)
+
+    def wt_copies(at):
+        cols = pl.ds(pl.multiple_of(at * width, width), width)
+        return [pltpu.make_async_copy(hbm.at[:, cols], wt_ref.at[at % 2, which], wt_sem.at[at % 2, which]) for which, hbm in enumerate((wq_hbm, wk_hbm, wv_hbm))]
+
+    def wo_copy(at):
+        cols = pl.ds(pl.multiple_of(at * tile, tile), tile)
+        return pltpu.make_async_copy(wo_hbm.at[:, cols], wo_ref.at[at % 2], wo_sem.at[at % 2])
+
+    @pl.when(step == 0)
+    def _():
+        y_copy = pltpu.make_async_copy(y_hbm, y_ref, y_sem)
+        y_copy.start()
+        for copy in wt_copies(0):
+            copy.start()
+        y_copy.wait()
         strip = 32
 
-        def norm_strip(step, carry):
-            rows = pl.ds(pl.multiple_of(step * strip, strip), strip)
+        def norm_strip(at, carry):
+            rows = pl.ds(pl.multiple_of(at * strip, strip), strip)
             y_wide = y_ref[rows, :].astype(jnp.float32)
             inv_rms = lax.rsqrt(jnp.mean(y_wide * y_wide, axis=-1, keepdims=True) + NORM_EPS)
             x_ref[rows, :] = (y_wide * inv_rms * norm_ref[...]).astype(x_ref.dtype)
             return carry
 
         lax.fori_loop(0, seq_len // strip, norm_strip, 0)
-
-    for wt_ref, dst_ref in ((wq_ref, q_ref), (wk_ref, k_ref), (wv_ref, v_ref)):
-        dst_ref[...] = jnp.dot(x_ref[...], wt_ref[...], preferred_element_type=jnp.float32).astype(dst_ref.dtype)
-
-    factor = (head_dim ** -0.5) * LOG2E
-    row_pos = lax.broadcasted_iota(jnp.int32, (block, block), 0)
-    col_pos = lax.broadcasted_iota(jnp.int32, (block, block), 1)
-    seen = row_pos >= col_pos
-    contract = (((1,), (1,)), ((), ()))
-    for head in range(out_ref.shape[1] // head_dim):
-        cols = slice(head * head_dim, (head + 1) * head_dim)
-        for part in range(2):
-            rows = slice(part * block, (part + 1) * block)
-            query = q_ref[rows, cols]
-            pieces = []
-            if part:
-                pieces.append(lax.dot_general(query, k_ref[:block, cols], contract, preferred_element_type=jnp.float32))
-            last = lax.dot_general(query, k_ref[rows, cols], contract, preferred_element_type=jnp.float32)
-            pieces.append(jnp.where(seen, last, -jnp.inf))
-            scores = jnp.concatenate(pieces, axis=1) if part else pieces[0]
-            top = jnp.max(scores, axis=1, keepdims=True)
-            grown = jnp.exp2((scores - top) * factor)
-            probs = (grown * (1.0 / jnp.sum(grown, axis=1, keepdims=True))).astype(jnp.bfloat16)
-            mixed = jnp.dot(probs, v_ref[:(part + 1) * block, cols], preferred_element_type=jnp.float32)
-            out_ref[rows, cols] = mixed.astype(out_ref.dtype)
-
-
-def attention(arrived, norm_w, weights, width):
+        for ref in (qb_ref, kb_ref, vb_ref):
+            ref[...] = jnp.zeros_like(ref)
+
+    @pl.when(step < steps)
+    def _():
+        @pl.when(step < steps - 1)
+        def _():
+            for copy in wt_copies(step + 1):
+                copy.start()
+
+        @pl.when(step == steps - 1)
+        def _():
+            wo_copy(0).start()
+
+        for copy in wt_copies(step):
+            copy.wait()
+        slot = step % 2
+
+        def emit(dst_refs, half, src_refs, base):
+            for which, dst_ref in enumerate(dst_refs):
+                wt = wt_ref[slot, which, :, half * pair:(half + 1) * pair]
+                dst_ref[...] = jnp.dot(x_ref[...], wt, preferred_element_type=jnp.float32).astype(dst_ref.dtype)
+                if which < 2:
+                    for part in range(2):
+                        rows, mixed = attend(*src_refs, which, part)
+                        attn_ref[rows, pl.ds(pl.multiple_of(base + which * LANES, LANES), LANES)] = mixed
+
+        first, second = (qa_ref, ka_ref, va_ref), (qb_ref, kb_ref, vb_ref)
+        before = jnp.where(step == 0, steps - 1, step - 1)
+        emit(first, 0, second, before * width + pair)
+        emit(second, 1, first, step * width)
+
+    @pl.when(step == steps)
+    def _():
+        for head in range(2):
+            for part in range(2):
+                rows, mixed = attend(qb_ref, kb_ref, vb_ref, head, part)
+                at = attn_ref.shape[1] - pair + head * LANES
+                attn_ref[rows, at:at + LANES] = mixed
+
+    @pl.when(step >= steps)
+    def _():
+        at = step - steps
+
+        @pl.when(at + 1 < d_model // tile)
+        def _():
+            wo_copy(at + 1).start()
+
+        wo_copy(at).wait()
+        proj = jnp.dot(attn_ref[...], wo_ref[at % 2], preferred_element_type=jnp.float32).astype(jnp.bfloat16)
+        y_tile = y_ref[:, pl.ds(pl.multiple_of(at * tile, tile), tile)]
+        out_ref[0, 0] = (y_tile.astype(jnp.float32) + proj.astype(jnp.float32)).astype(out_ref.dtype)
+
+
+def attention(micro, arrived, norm_w, weights, w_out, result, out_shape, width, tile):
     seq_len, d_model = arrived.shape
     depth = weights[0].shape[1]
-    wt_spec = pl.BlockSpec((d_model, width), lambda h: (0, h))
-    head_scratch = pltpu.VMEM((seq_len, width), jnp.bfloat16)
+    steps = depth // width
+    hbm = pl.BlockSpec(memory_space=pl.ANY)
+    operands = [norm_w, arrived, *weights, w_out]
+    aliases = {}
+    if result is not None:
+        operands.append(result)
+        aliases = {len(operands) - 1: 0}
+    head_pair = pltpu.VMEM((seq_len, width // 2), jnp.bfloat16)
     return pl.pallas_call(
         attention_kernel,
-        out_shape=jax.ShapeDtypeStruct((seq_len, depth), jnp.bfloat16),
-        grid=(depth // width,),
-        in_specs=[
-            pl.BlockSpec((seq_len, d_model), lambda h: (0, 0)),
-            pl.BlockSpec((1, d_model), lambda h: (0, 0)),
-            wt_spec, wt_spec, wt_spec,
+        out_shape=jax.ShapeDtypeStruct(out_shape, jnp.bfloat16),
+        grid=(steps + d_model // tile,),
+        in_specs=[pl.BlockSpec((1, d_model), lambda h: (0, 0))] + [hbm] * (len(operands) - 1),
+        out_specs=pl.BlockSpec((1, 1, seq_len, tile), lambda h: (micro, 0, 0, jnp.maximum(h - steps, 0))),
+        scratch_shapes=[
+            pltpu.VMEM((seq_len, d_model), jnp.bfloat16),
+            pltpu.VMEM((seq_len, d_model), jnp.bfloat16),
+            pltpu.VMEM((seq_len, depth), jnp.bfloat16),
+            pltpu.VMEM((2, 3, d_model, width), jnp.bfloat16),
+            pltpu.VMEM((2, depth, tile), jnp.bfloat16),
+            *[head_pair] * 6,
+            pltpu.SemaphoreType.DMA,
+            pltpu.SemaphoreType.DMA((2, 3)),
+            pltpu.SemaphoreType.DMA((2,)),
         ],
-        out_specs=pl.BlockSpec((seq_len, width), lambda h: (0, h)),
-        scratch_shapes=[pltpu.VMEM((seq_len, d_model), jnp.bfloat16), head_scratch, head_scratch, head_scratch],
-        compiler_params=pltpu.CompilerParams(vmem_limit_bytes=60 << 20),
-        cost_estimate=pl.CostEstimate(flops=6 * seq_len * d_model * depth, bytes_accessed=6 * d_model * depth, transcendentals=0),
-        name='attention',
-    )(arrived, norm_w, *weights)
-
-
-def project_kernel(attn_ref, wt_ref, res_ref, *refs):
-    out_ref = refs[-1]
-    proj = jnp.dot(attn_ref[...], wt_ref[...], preferred_element_type=jnp.float32).astype(jnp.bfloat16)
-    out_ref[0, 0] = (res_ref[...].astype(jnp.float32) + proj.astype(jnp.float32)).astype(out_ref.dtype)
-
-
-def project(micro, attn_out, w_out, arrived, result, out_shape, tile):
-    tokens, depth = attn_out.shape
-    d_model = w_out.shape[1]
-    in_specs = [
-        pl.BlockSpec((tokens, depth), lambda n: (0, 0)),
-        pl.BlockSpec((depth, tile), lambda n: (0, n)),
-        pl.BlockSpec((tokens, tile), lambda n: (0, n)),
-    ]
-    operands = [attn_out, w_out, arrived]
-    aliases = {}
-    if result is not None:
-        in_specs.append(pl.BlockSpec(memory_space=pl.ANY))
-        operands.append(result)
-        aliases = {3: 0}
-    return pl.pallas_call(
-        project_kernel,
-        out_shape=jax.ShapeDtypeStruct(out_shape, jnp.bfloat16),
-        grid=(d_model // tile,),
-        in_specs=in_specs,
-        out_specs=pl.BlockSpec((1, 1, tokens, tile), lambda n: (micro, 0, 0, n)),
         input_output_aliases=aliases,
         compiler_params=pltpu.CompilerParams(vmem_limit_bytes=60 << 20),
-        cost_estimate=pl.CostEstimate(flops=2 * tokens * depth * d_model, bytes_accessed=2 * depth * d_model, transcendentals=0),
-        name='project',
+        cost_estimate=pl.CostEstimate(flops=8 * seq_len * d_model * depth, bytes_accessed=8 * d_model * depth, transcendentals=0),
+        name='attention',
     )(*operands)
 
 
@@ -276,7 +327,7 @@
             for micro, row in zip(micros, rows):
                 arrived.append(lax.ppermute(row, 'pp', send_next))
         raw = lax.optimization_barrier((w_query, w_key, w_value, combined[-1]))[:3]
-        weights = [regroup(wt, 256, 8) for wt in raw]
+        weights = [regroup(wt, 1024, 8) for wt in raw]
 
         flat_out = w_out[0].reshape(-1, d_model)
         result = None
@@ -284,8 +335,7 @@
             rows = arrived[micro]
             if micro:
                 rows, result = lax.optimization_barrier((rows, result))
-            attn_out = attention(rows, norm_w, weights, 512)
-            result = project(micro, attn_out, flat_out, rows, result, residual.shape, 512)
+            result = attention(micro, rows, norm_w, weights, flat_out, result, residual.shape, 512, 512)
         return result
 
     return jax.shard_map(device_step, mesh=mesh, in_specs=(tok_spec, tok_spec, tok_spec, tok_spec, tok_spec, P('pp', None), wt_spec, wt_spec, wt_spec, wt_spec), out_specs=tok_spec, check_vma=False)

time: 956 us -> 933 us (0.976)
  Pallas kernels: 936 us -> 915 us
    pallas_call x3, Pallas kernels: 154 us -> 103 us  [regroup(): pl.pallas_call(regroup_kernel, out_shape=jax.ShapeDtypeStruct((d_model, n...]
    pallas_call x12 -> x6, Pallas kernels: 684 us -> 713 us  [attention(): pl.pallas_call(attention_kernel, out_shape=jax.ShapeDtypeStruct(out_shape...]
  transfers between devices with their start and end apart: 6 -> 6, of which waited for: 0 -> 0; matrix products, arithmetic and copies ran while one was open for 0% -> 0% of each run, Pallas kernels for 85% -> 84%
where the time goes in v2:
time: 933 us; the launch traced here: 923 us
  Pallas kernels  915 us (98%)
    pallas_call x6, Pallas kernels, attention(): pl.pallas_call(attention_kernel, out_shape=jax.ShapeDtypeStruct(out_shape...  713 us
    pallas_call x3, Pallas kernels, regroup(): pl.pallas_call(regroup_kernel, out_shape=jax.ShapeDtypeStruct((d_model, n...  103 us
    pallas_call x3, Pallas kernels, combine(): pl.pallas_call(functools.partial(combine_kernel, micros), out_shape=[jax....  98.4 us
  transfers between devices with their start and end apart: 6, of which 0 were waited for; matrix products, arithmetic and copies ran while one was open for 0% of the time, Pallas kernels for 84%

profile of v2, /device:TPU:4, one launch (start us, length us, event | category | flops | bytes accessed | tf_op | source)
XLA Modules:
  0.0 923.0 jit_solution(1249465836728083027)
XLA Ops:
  0.0 1.4 fusion.key_ref
  1.4 17.2 %combine.3 = bf16[512,4096]{1,0:T(8,128)(2,1)} custom-call(s32[6,2,512]{2,1,0:T(2,128)} %fusion.key_ref, f32[6,2,512]{2,1,0:T(2,128)} %bitcast.21, bf16[6,4,320,4096]{3,2,1,0:T(8,128)(2,1)} %expert_ref.5, bf16[6,1,512,4096]{3,2,1,0:T(8,128)(2,1)} %res_ref.5), custom_call_target="tpu_custom_call" | custom-call | flops 10737418240 | bytes 18874368 | tf_op jit(solution)/shard_map/combine/pallas_call | solution.py:104
  18.7 1.5 collective-permute-start.5
  20.2 32.8 %combine.4 = (bf16[512,4096]{1,0:T(8,128)(2,1)}, bf16[512,4096]{1,0:T(8,128)(2,1)}) custom-call(s32[6,2,512]{2,1,0:T(2,128)} %fusion.key_ref, f32[6,2,512]{2,1,0:T(2,128)} %bitcast.22, bf16[6,4,320,4096]{3,2,1,0:T(8,128)(2,1)} %expert_ref.5, bf16[6,1,512,4096]{3,2,1,0:T(8,128)(2,1)} %res_ref.5), custom_call_target="tpu_custom_call" | custom-call | flops 21474836480 | bytes 37748736 | tf_op jit(solution)/shard_map/combine/pallas_call | solution.py:104
  53.0 0.1 collective-permute-start.4
  53.1 1.9 collective-permute-start.3
  55.0 48.3 %combine.5 = (bf16[512,4096]{1,0:T(8,128)(2,1)}, bf16[512,4096]{1,0:T(8,128)(2,1)}, bf16[512,4096]{1,0:T(8,128)(2,1)}) custom-call(s32[6,2,512]{2,1,0:T(2,128)} %fusion.key_ref, f32[6,2,512]{2,1,0:T(2,128)} %bitcast.23, bf16[6,4,320,4096]{3,2,1,0:T(8,128)(2,1)} %expert_ref.5, bf16[6,1,512,4096]{3,2,1,0:T(8,128)(2,1)} %res_ref.5), custom_call_target="tpu_custom_call" | custom-call | flops 32212254720 | bytes 56623104 | tf_op jit(solution)/shard_map/combine/pallas_call | solution.py:104
  103.3 1.5 collective-permute-start.1
  104.9 1.5 collective-permute-start
  106.3 34.3 %regroup.3.wq_hbm = bf16[4096,4096]{1,0:T(8,128)(2,1)} custom-call(bf16[1,4096,32,128]{3,2,1,0:T(8,128)(2,1)} %wt_ref), custom_call_target="tpu_custom_call" | custom-call | flops 10000000000 | bytes 67108864 | tf_op jit(solution)/shard_map/regroup/pallas_call | solution.py:145
  140.7 34.4 %regroup.4.wk_hbm = bf16[4096,4096]{1,0:T(8,128)(2,1)} custom-call(bf16[1,4096,32,128]{3,2,1,0:T(8,128)(2,1)} %wt_ref.1), custom_call_target="tpu_custom_call" | custom-call | flops 10000000000 | bytes 67108864 | tf_op jit(solution)/shard_map/regroup/pallas_call | solution.py:145
  175.0 34.4 %regroup.5.wv_hbm = bf16[4096,4096]{1,0:T(8,128)(2,1)} custom-call(bf16[1,4096,32,128]{3,2,1,0:T(8,128)(2,1)} %wt_ref.2), custom_call_target="tpu_custom_call" | custom-call | flops 10000000000 | bytes 67108864 | tf_op jit(solution)/shard_map/regroup/pallas_call | solution.py:145
  209.4 0.0 collective-permute-done.5.y_hbm
  209.4 0.1 collective-permute-start.2
  209.5 118.8 %attention.6.refs_0_ = bf16[6,1,512,4096]{3,2,1,0:T(8,128)(2,1)} custom-call(f32[1,4096]{1,0:T(1,128)} %norm_ref.11, bf16[512,4096]{1,0:T(8,128)(2,1)} %collective-permute-done.5.y_hbm, bf16[4096,4096]{1,0:T(8,128)(2,1)} %regroup.3.wq_hbm, bf16[4096,4096]{1,0:T(8,128)(2,1)} %regroup.4.wk_hbm, bf16[4096,4096]{1,0:T(8,128)(2,1)} %regroup.5.wv_hbm, ...), custom_call_target="tpu_custom_call" | custom-call | flops 68719476736 | bytes 134217728 | tf_op jit(solution)/shard_map/attention/pallas_call | solution.py:277
  328.2 0.0 collective-permute-done.4.y_hbm
  328.3 118.8 %attention.7.refs_0_ = bf16[6,1,512,4096]{3,2,1,0:T(8,128)(2,1)} custom-call(f32[1,4096]{1,0:T(1,128)} %norm_ref.11, bf16[512,4096]{1,0:T(8,128)(2,1)} %collective-permute-done.4.y_hbm, bf16[4096,4096]{1,0:T(8,128)(2,1)} %regroup.3.wq_hbm, bf16[4096,4096]{1,0:T(8,128)(2,1)} %regroup.4.wk_hbm, ...), custom_call_target="tpu_custom_call", output_to_operand_aliasing={{}: (6, {})} | custom-call | flops 68719476736 | bytes 134217728 | tf_op jit(solution)/shard_map/attention/pallas_call | solution.py:277
  447.1 0.0 collective-permute-done.3.y_hbm
  447.1 119.0 %attention.8.refs_0_ = bf16[6,1,512,4096]{3,2,1,0:T(8,128)(2,1)} custom-call(f32[1,4096]{1,0:T(1,128)} %norm_ref.11, bf16[512,4096]{1,0:T(8,128)(2,1)} %collective-permute-done.3.y_hbm, bf16[4096,4096]{1,0:T(8,128)(2,1)} %regroup.3.wq_hbm, bf16[4096,4096]{1,0:T(8,128)(2,1)} %regroup.4.wk_hbm, ...), custom_call_target="tpu_custom_call", output_to_operand_aliasing={{}: (6, {})} | custom-call | flops 68719476736 | bytes 134217728 | tf_op jit(solution)/shard_map/attention/pallas_call | solution.py:277
  566.1 0.0 collective-permute-done.2.y_hbm
  566.2 118.8 %attention.9.refs_0_ = bf16[6,1,512,4096]{3,2,1,0:T(8,128)(2,1)} custom-call(f32[1,4096]{1,0:T(1,128)} %norm_ref.11, bf16[512,4096]{1,0:T(8,128)(2,1)} %collective-permute-done.2.y_hbm, bf16[4096,4096]{1,0:T(8,128)(2,1)} %regroup.3.wq_hbm, bf16[4096,4096]{1,0:T(8,128)(2,1)} %regroup.4.wk_hbm, ...), custom_call_target="tpu_custom_call", output_to_operand_aliasing={{}: (6, {})} | custom-call | flops 68719476736 | bytes 134217728 | tf_op jit(solution)/shard_map/attention/pallas_call | solution.py:277
  685.0 0.0 collective-permute-done.1.y_hbm
  685.0 118.8 %attention.10.refs_0_ = bf16[6,1,512,4096]{3,2,1,0:T(8,128)(2,1)} custom-call(f32[1,4096]{1,0:T(1,128)} %norm_ref.11, bf16[512,4096]{1,0:T(8,128)(2,1)} %collective-permute-done.1.y_hbm, bf16[4096,4096]{1,0:T(8,128)(2,1)} %regroup.3.wq_hbm, bf16[4096,4096]{1,0:T(8,128)(2,1)} %regroup.4.wk_hbm, ...), custom_call_target="tpu_custom_call", output_to_operand_aliasing={{}: (6, {})} | custom-call | flops 68719476736 | bytes 134217728 | tf_op jit(solution)/shard_map/attention/pallas_call | solution.py:277
  803.8 0.0 collective-permute-done.y_hbm
  803.8 118.9 %attention.11 = bf16[6,1,512,4096]{3,2,1,0:T(8,128)(2,1)} custom-call(f32[1,4096]{1,0:T(1,128)} %norm_ref.11, bf16[512,4096]{1,0:T(8,128)(2,1)} %collective-permute-done.y_hbm, bf16[4096,4096]{1,0:T(8,128)(2,1)} %regroup.3.wq_hbm, bf16[4096,4096]{1,0:T(8,128)(2,1)} %regroup.4.wk_hbm, ...), custom_call_target="tpu_custom_call", output_to_operand_aliasing={{}: (6, {})} | custom-call | flops 68719476736 | bytes 134217728 | tf_op jit(solution)/shard_map/attention/pallas_call | solution.py:277
Async XLA Ops:
  18.7 190.7 %collective-permute-start.5 = (bf16[512,4096]{1,0:T(8,128)(2,1)}, bf16[512,4096]{1,0:T(8,128)(2,1)}, u32[]{:S(2)}, u32[]{:S(2)}) collective-permute-start(bf16[512,4096]{1,0:T(8,128)(2,1)} %combine.3), channel_id=1, source_target_pairs={{0,2},{2,4},{4,6},{6,0},{1,3},{3,5},{5,7},{7,1}} | collective-permute-start | bytes 12582920 | tf_op jit(solution)/shard_map/ppermute | solution.py:328
  53.0 275.3 %collective-permute-start.4 = (bf16[512,4096]{1,0:T(8,128)(2,1)}, bf16[512,4096]{1,0:T(8,128)(2,1)}, u32[]{:S(2)}, u32[]{:S(2)}) collective-permute-start(bf16[512,4096]{1,0:T(8,128)(2,1)} %get-tuple-element.31), channel_id=1, source_target_pairs={{0,2},{2,4},{4,6},{6,0},{1,3},{3,5},{5,7},{7,1}} | collective-permute-start | bytes 12582920 | tf_op jit(solution)/shard_map/ppermute | solution.py:328
  53.1 394.0 %collective-permute-start.3 = (bf16[512,4096]{1,0:T(8,128)(2,1)}, bf16[512,4096]{1,0:T(8,128)(2,1)}, u32[]{:S(2)}, u32[]{:S(2)}) collective-permute-start(bf16[512,4096]{1,0:T(8,128)(2,1)} %get-tuple-element.26), channel_id=1, source_target_pairs={{0,2},{2,4},{4,6},{6,0},{1,3},{3,5},{5,7},{7,1}} | collective-permute-start | bytes 12582920 | tf_op jit(solution)/shard_map/ppermute | solution.py:328
  103.3 581.6 %collective-permute-start.1 = (bf16[512,4096]{1,0:T(8,128)(2,1)}, bf16[512,4096]{1,0:T(8,128)(2,1)}, u32[]{:S(2)}, u32[]{:S(2)}) collective-permute-start(bf16[512,4096]{1,0:T(8,128)(2,1)} %get-tuple-element.29), channel_id=1, source_target_pairs={{0,2},{2,4},{4,6},{6,0},{1,3},{3,5},{5,7},{7,1}} | collective-permute-start | bytes 12582920 | tf_op jit(solution)/shard_map/ppermute | solution.py:328
  104.9 699.0 %collective-permute-start = (bf16[512,4096]{1,0:T(8,128)(2,1)}, bf16[512,4096]{1,0:T(8,128)(2,1)}, u32[]{:S(2)}, u32[]{:S(2)}) collective-permute-start(bf16[512,4096]{1,0:T(8,128)(2,1)} %get-tuple-element.28), channel_id=1, source_target_pairs={{0,2},{2,4},{4,6},{6,0},{1,3},{3,5},{5,7},{7,1}} | collective-permute-start | bytes 12582920 | tf_op jit(solution)/shard_map/ppermute | solution.py:328
  209.4 356.7 %collective-permute-start.2 = (bf16[512,4096]{1,0:T(8,128)(2,1)}, bf16[512,4096]{1,0:T(8,128)(2,1)}, u32[]{:S(2)}, u32[]{:S(2)}) collective-permute-start(bf16[512,4096]{1,0:T(8,128)(2,1)} %get-tuple-element.30), channel_id=1, source_target_pairs={{0,2},{2,4},{4,6},{6,0},{1,3},{3,5},{5,7},{7,1}} | collective-permute-start | bytes 12582920 | tf_op jit(solution)/shard_map/ppermute | solution.py:328

commit v3 on v2

v3 whole, which is shorter than its diff:
```python
import functools

import jax
import jax.numpy as jnp
from jax import lax
from jax.experimental import pallas as pl
from jax.experimental.pallas import tpu as pltpu
from jax.sharding import PartitionSpec as P


NORM_EPS = 1e-6
LOG2E = 1.4426950408889634
LANES = 128


def combine_kernel(micros, key_ref, gate_ref, expert_ref, res_ref, *refs):
    count = len(micros)
    out_refs = refs[:count]
    table_ref, pick_ref, wide_ref, own_sem, send_sem, recv_sem = refs[count:]
    slots = table_ref.shape[0]
    experts, src_slots, span = table_ref.shape[1] // 2, table_ref.shape[2], table_ref.shape[3]
    halves, tokens, width = slots // count, out_refs[0].shape[0], out_refs[0].shape[1]
    per_slot = span // width
    depth = pick_ref.shape[1]
    block = tokens // 2
    step, tile = pl.program_id(0), pl.program_id(1)
    slot = step * halves + tile // per_slot
    me = lax.axis_index('ep')
    mate = 1 - me

    def own_rows(slot):
        cols = pl.ds(pl.multiple_of(slot % halves * span, span), span)
        rows = pl.ds(pl.multiple_of(me * src_slots, src_slots), src_slots)
        return pltpu.make_async_copy(expert_ref.at[micros[0] + slot // halves, :, rows, cols], table_ref.at[slot, :experts], own_sem.at[slot])

    def mate_rows(slot):
        cols = pl.ds(pl.multiple_of(slot % halves * span, span), span)
        rows = pl.ds(pl.multiple_of(mate * src_slots, src_slots), src_slots)
        return pltpu.make_async_remote_copy(
            src_ref=expert_ref.at[micros[0] + slot // halves, :, rows, cols],
            dst_ref=table_ref.at[slot, experts:],
            send_sem=send_sem.at[slot],
            recv_sem=recv_sem.at[slot],
            device_id={'ep': mate},
            device_id_type=pl.DeviceIdType.MESH,
        )

    @pl.when((step == 0) & (tile == 0))
    def _():
        barrier = pltpu.get_barrier_semaphore()
        pl.semaphore_signal(barrier, inc=1, device_id={'ep': mate}, device_id_type=pl.DeviceIdType.MESH)
        own_rows(0).start()
        pl.semaphore_wait(barrier, 1)
        mate_rows(0).start()
        for at in range(1, slots):
            mate_rows(at).start()
            own_rows(at).start()

    @pl.when(tile == 0)
    def _():
        for choice in range(2):
            gates = jnp.broadcast_to(gate_ref[0, choice:choice + 1, :], (LANES, tokens)).T
            keys = jnp.broadcast_to(key_ref[0, choice:choice + 1, :], (LANES, tokens)).T
            lane = lax.broadcasted_iota(jnp.int32, (block, LANES), 1)
            for half in range(2):
                src = slice(half * block, (half + 1) * block)
                rows = slice((2 * half + choice) * block, (2 * half + choice + 1) * block)
                wide_ref[rows] = gates[src]
                for col in range(0, depth, LANES):
                    pick_ref[rows, col:col + LANES] = jnp.where(keys[src] == lane + col, 1.0, 0.0).astype(pick_ref.dtype)

    @pl.when(tile % per_slot == 0)
    def _():
        own_rows(slot).wait()
        arriving = mate_rows(slot)
        arriving.wait_recv()
        arriving.wait_send()

    table = table_ref[slot, :, :, pl.ds(pl.multiple_of(tile % per_slot * width, width), width)].reshape(depth, width)
    mixed = []
    for half in range(2):
        base = 2 * half * block
        picked = jnp.dot(pick_ref[base:base + 2 * block], table, preferred_element_type=jnp.float32)
        first, second = wide_ref[base:base + block], wide_ref[base + block:base + 2 * block]
        strips = []
        for col in range(0, width, LANES):
            cols = slice(col, col + LANES)
            gated = first * picked[:block, cols] + second * picked[block:, cols]
            strips.append((res_ref[0, 0, half * block:(half + 1) * block, cols].astype(jnp.float32) + gated).astype(jnp.bfloat16))
        mixed.append(jnp.concatenate(strips, axis=1))
    for at, out_ref in enumerate(out_refs):
        @pl.when(step == at)
        def _(out_ref=out_ref):
            for half in range(2):
                out_ref[half * block:(half + 1) * block] = mixed[half]


def combine(micros, call_id, keys, gates, expert_out, residual, width):
    _, experts, capacity, d_model = expert_out.shape
    src_slots = capacity // 2
    tokens = residual.shape[2]
    depth = 2 * experts * src_slots
    count, tiles, base = len(micros), d_model // width, micros[0]
    slots = 2 * count

    def out_spec(at):
        return pl.BlockSpec((tokens, width), lambda m, n: (0, jnp.where(m < at, 0, jnp.where(m > at, tiles - 1, n))))

    return pl.pallas_call(
        functools.partial(combine_kernel, micros),
        out_shape=[jax.ShapeDtypeStruct((tokens, d_model), jnp.bfloat16)] * count,
        grid=(count, tiles),
        in_specs=[
            pl.BlockSpec((1, 2, tokens), lambda m, n: (base + m, 0, 0)),
            pl.BlockSpec((1, 2, tokens), lambda m, n: (base + m, 0, 0)),
            pl.BlockSpec(memory_space=pl.ANY),
            pl.BlockSpec((1, 1, tokens, width), lambda m, n: (base + m, 0, 0, n)),
        ],
        out_specs=[out_spec(at) for at in range(count)],
        scratch_shapes=[
            pltpu.VMEM((slots, 2 * experts, src_slots, d_model * count // slots), jnp.bfloat16),
            pltpu.VMEM((2 * tokens, depth), jnp.bfloat16),
            pltpu.VMEM((2 * tokens, LANES), jnp.float32),
            pltpu.SemaphoreType.DMA((slots,)),
            pltpu.SemaphoreType.DMA((slots,)),
            pltpu.SemaphoreType.DMA((slots,)),
        ],
        compiler_params=pltpu.CompilerParams(vmem_limit_bytes=60 << 20, collective_id=call_id, has_side_effects=True),
        cost_estimate=pl.CostEstimate(flops=4 * count * tokens * depth * d_model, bytes_accessed=2 * count * d_model * (depth + 2 * tokens), transcendentals=0),
        name='combine',
    )(keys, gates, expert_out, residual)


def regroup_kernel(wt_ref, out_ref, wide_ref):
    _, rows, width = out_ref.shape
    head_dim = wt_ref.shape[3]
    sub = wide_ref.shape[1] // rows
    per_group = width // head_dim
    for at in range(wt_ref.shape[2] // sub):
        wide = wide_ref.at[at % 2]
        wide[...] = wt_ref[0, :, at * sub:(at + 1) * sub].astype(jnp.float32).reshape(rows * sub, head_dim)
        for head in range(sub):
            group, place = divmod(at * sub + head, per_group)
            out_ref[group, :, place * head_dim:(place + 1) * head_dim] = wide[pl.ds(head, rows, stride=sub), :].astype(out_ref.dtype)


def regroup(weight, rows, width):
    _, d_model, num_heads, head_dim = weight.shape
    groups = num_heads * head_dim // width
    sub = 8
    return pl.pallas_call(
        regroup_kernel,
        out_shape=jax.ShapeDtypeStruct((groups, d_model, width), weight.dtype),
        grid=(d_model // rows,),
        in_specs=[pl.BlockSpec((1, rows, num_heads, head_dim), lambda r: (0, r, 0, 0))],
        out_specs=pl.BlockSpec((groups, rows, width), lambda r: (0, r, 0)),
        scratch_shapes=[pltpu.VMEM((2, rows * sub, head_dim), jnp.float32)],
        compiler_params=pltpu.CompilerParams(vmem_limit_bytes=60 << 20),
        cost_estimate=pl.CostEstimate(flops=10 ** 10, bytes_accessed=4 * d_model * num_heads * head_dim, transcendentals=0),
        name='regroup',
    )(weight)


def attend(q_ref, k_ref, v_ref, head, part):
    seq_len, head_dim = q_ref.shape[0], LANES
    block = seq_len // 2
    cols = slice(head * head_dim, (head + 1) * head_dim)
    rows = slice(part * block, (part + 1) * block)
    contract = (((1,), (1,)), ((), ()))
    query = q_ref[rows, cols]
    seen = lax.broadcasted_iota(jnp.int32, (block, block), 0) >= lax.broadcasted_iota(jnp.int32, (block, block), 1)
    last = lax.dot_general(query, k_ref[rows, cols], contract, preferred_element_type=jnp.float32)
    scores = jnp.where(seen, last, -jnp.inf)
    if part:
        early = lax.dot_general(query, k_ref[:block, cols], contract, preferred_element_type=jnp.float32)
        scores = jnp.concatenate([early, scores], axis=1)
    top = jnp.max(scores, axis=1, keepdims=True)
    grown = jnp.exp2((scores - top) * ((head_dim ** -0.5) * LOG2E))
    probs = (grown * (1.0 / jnp.sum(grown, axis=1, keepdims=True))).astype(jnp.bfloat16)
    mixed = jnp.dot(probs, v_ref[:(part + 1) * block, cols], preferred_element_type=jnp.float32)
    return rows, mixed.astype(jnp.bfloat16)


def attention_kernel(norm_ref, y_hbm, wq_hbm, wk_hbm, wv_hbm, wo_hbm, *refs):
    out_ref, y_ref, x_ref, attn_ref, wt_ref, wo_ref, *head_refs, y_sem, wt_sem, wo_sem = refs[-15:]
    fresh, ready = head_refs[:3], head_refs[3:]
    seq_len, d_model = y_ref.shape
    depth = attn_ref.shape[1]
    steps, _, width = wq_hbm.shape
    tile = wo_ref.shape[2]
    units = [(head, part) for head in range(width // LANES) for part in range(2)]
    step = pl.program_id(0)

    def wt_copies(at):
        return [pltpu.make_async_copy(hbm.at[at], wt_ref.at[at % 2, which], wt_sem.at[at % 2, which]) for which, hbm in enumerate((wq_hbm, wk_hbm, wv_hbm))]

    def wo_copy(at):
        cols = pl.ds(pl.multiple_of(at * tile, tile), tile)
        return pltpu.make_async_copy(wo_hbm.at[:, cols], wo_ref.at[at % 2], wo_sem.at[at % 2])

    def finish(at, proj):
        y_tile = y_ref[:, pl.ds(pl.multiple_of(at * tile, tile), tile)]
        rounded = proj.astype(jnp.bfloat16).astype(jnp.float32)
        out_ref[0, 0] = (y_tile.astype(jnp.float32) + rounded).astype(out_ref.dtype)

    @pl.when(step == 0)
    def _():
        y_copy = pltpu.make_async_copy(y_hbm, y_ref, y_sem)
        y_copy.start()
        for copy in wt_copies(0):
            copy.start()
        y_copy.wait()
        strip = 32

        def norm_strip(at, carry):
            rows = pl.ds(pl.multiple_of(at * strip, strip), strip)
            y_wide = y_ref[rows, :].astype(jnp.float32)
            inv_rms = lax.rsqrt(jnp.mean(y_wide * y_wide, axis=-1, keepdims=True) + NORM_EPS)
            x_ref[rows, :] = (y_wide * inv_rms * norm_ref[...]).astype(x_ref.dtype)
            return carry

        lax.fori_loop(0, seq_len // strip, norm_strip, 0)
        for ref in ready:
            ref[...] = jnp.zeros_like(ref)

    @pl.when(step < steps)
    def _():
        @pl.when(step < steps - 1)
        def _():
            for copy in wt_copies(step + 1):
                copy.start()

        @pl.when(step == steps - 1)
        def _():
            wo_copy(0).start()

        for copy in wt_copies(step):
            copy.wait()
        slot = step % 2
        base = jnp.where(step == 0, steps - 1, step - 1) * width
        share = (len(units) + 2) // 3
        for which in range(3):
            fresh[which][...] = jnp.dot(x_ref[...], wt_ref[slot, which], preferred_element_type=jnp.float32).astype(jnp.bfloat16)
            for head, part in units[which * share:(which + 1) * share]:
                rows, mixed = attend(*ready, head, part)
                attn_ref[rows, pl.ds(pl.multiple_of(base + head * LANES, LANES), LANES)] = mixed
        for src_ref, dst_ref in zip(fresh, ready):
            dst_ref[...] = src_ref[...]

    @pl.when(step == steps)
    def _():
        wo_copy(1).start()
        wo_copy(0).wait()
        early = depth - width
        proj = jnp.dot(attn_ref[:, :early], wo_ref[0, :early], preferred_element_type=jnp.float32)
        for head, part in units:
            rows, mixed = attend(*ready, head, part)
            attn_ref[rows, early + head * LANES:early + (head + 1) * LANES] = mixed
        finish(0, proj + jnp.dot(attn_ref[:, early:], wo_ref[0, early:], preferred_element_type=jnp.float32))

    @pl.when(step > steps)
    def _():
        at = step - steps

        @pl.when(at + 1 < d_model // tile)
        def _():
            wo_copy(at + 1).start()

        wo_copy(at).wait()
        finish(at, jnp.dot(attn_ref[...], wo_ref[at % 2], preferred_element_type=jnp.float32))


def attention(micro, arrived, norm_w, weights, w_out, result, out_shape, tile):
    seq_len, d_model = arrived.shape
    steps, _, width = weights[0].shape
    depth = steps * width
    hbm = pl.BlockSpec(memory_space=pl.ANY)
    operands = [norm_w, arrived, *weights, w_out]
    aliases = {}
    if result is not None:
        operands.append(result)
        aliases = {len(operands) - 1: 0}
    head_group = pltpu.VMEM((seq_len, width), jnp.bfloat16)
    return pl.pallas_call(
        attention_kernel,
        out_shape=jax.ShapeDtypeStruct(out_shape, jnp.bfloat16),
        grid=(steps + d_model // tile,),
        in_specs=[pl.BlockSpec((1, d_model), lambda h: (0, 0))] + [hbm] * (len(operands) - 1),
        out_specs=pl.BlockSpec((1, 1, seq_len, tile), lambda h: (micro, 0, 0, jnp.maximum(h - steps, 0))),
        scratch_shapes=[
            pltpu.VMEM((seq_len, d_model), jnp.bfloat16),
            pltpu.VMEM((seq_len, d_model), jnp.bfloat16),
            pltpu.VMEM((seq_len, depth), jnp.bfloat16),
            pltpu.VMEM((2, 3, d_model, width), jnp.bfloat16),
            pltpu.VMEM((2, depth, tile), jnp.bfloat16),
            *[head_group] * 6,
            pltpu.SemaphoreType.DMA,
            pltpu.SemaphoreType.DMA((2, 3)),
            pltpu.SemaphoreType.DMA((2,)),
        ],
        input_output_aliases=aliases,
        compiler_params=pltpu.CompilerParams(vmem_limit_bytes=60 << 20),
        cost_estimate=pl.CostEstimate(flops=8 * seq_len * d_model * depth, bytes_accessed=8 * d_model * depth, transcendentals=0),
        name='attention',
    )(*operands)


def solution(mesh):
    stages = mesh.shape['pp']
    group_size = mesh.shape['ep']
    send_next = [(src, (src + 1) % stages) for src in range(stages)]
    tok_spec = P('pp', 'ep', None, None)
    wt_spec = P('pp', None, None, None)

    def device_step(expert_out, expert_ids, slot_ids, gate_vals, residual, norm_w, w_query, w_key, w_value, w_out):
        num_micro, _, _, d_model = residual.shape
        experts, capacity = expert_out.shape[1:3]
        src_slots = capacity // group_size
        num_experts = experts * group_size
        position = lax.axis_index('ep').astype(jnp.int32)

        place = (expert_ids[:, 0] - position * experts) % num_experts
        keys = jnp.where(slot_ids[:, 0] >= 0, place * src_slots + slot_ids[:, 0] - position * src_slots, -1)
        keys = jnp.swapaxes(keys, 1, 2)
        gates = jnp.swapaxes(gate_vals[:, 0], 1, 2)

        arrived = []
        combined = []
        for call_id, micros in enumerate(((0,), (1, 2), (3, 4, 5))):
            if combined:
                keys = lax.optimization_barrier((keys, combined[-1]))[0]
            rows = combine(micros, call_id, keys, gates, expert_out, residual, 512)
            combined.extend(rows)
            for micro, row in zip(micros, rows):
                arrived.append(lax.ppermute(row, 'pp', send_next))
        raw = lax.optimization_barrier((w_query, w_key, w_value, combined[-1]))[:3]
        weights = [regroup(wt, 256, 512) for wt in raw]

        flat_out = w_out[0].reshape(-1, d_model)
        result = None
        for micro in range(num_micro):
            rows = arrived[micro]
            if micro:
                rows, result = lax.optimization_barrier((rows, result))
            result = attention(micro, rows, norm_w, weights, flat_out, result, residual.shape, 512)
        return result

    return jax.shard_map(device_step, mesh=mesh, in_specs=(tok_spec, tok_spec, tok_spec, tok_spec, tok_spec, P('pp', None), wt_spec, wt_spec, wt_spec, wt_spec), out_specs=tok_spec, check_vma=False)
```

time: 933 us -> 913 us (0.979)
  Pallas kernels: 915 us -> 880 us
  waiting for transfers between devices: 0.02 us -> 13.4 us
    pallas_call x6, Pallas kernels: 713 us -> 675 us  [attention(): pl.pallas_call(attention_kernel, out_shape=jax.ShapeDtypeStruct(out_shape...]
    ppermute x6, waiting for transfers between devices: 0.02 us -> 13.4 us  [device_step(): arrived.append(lax.ppermute(row, 'pp', send_next))]
  transfers between devices with their start and end apart: 6 -> 6, of which waited for: 0 -> 1; matrix products, arithmetic and copies ran while one was open for 0% -> 0% of each run, Pallas kernels for 84% -> 83%
where the time goes in v3:
time: 913 us; the launch traced here: 902 us
  Pallas kernels  880 us (96%)
  waiting for transfers between devices  13.4 us (1%)
    pallas_call x6, Pallas kernels, attention(): pl.pallas_call(attention_kernel, out_shape=jax.ShapeDtypeStruct(out_shape...  675 us
    pallas_call x3, Pallas kernels, combine(): pl.pallas_call(functools.partial(combine_kernel, micros), out_shape=[jax....  106 us
    pallas_call x3, Pallas kernels, regroup(): pl.pallas_call(regroup_kernel, out_shape=jax.ShapeDtypeStruct((groups, d_...  100 us
  transfers between devices with their start and end apart: 6, of which 1 were waited for; matrix products, arithmetic and copies ran while one was open for 0% of the time, Pallas kernels for 83%

profile of v3, /device:TPU:4, one launch (start us, length us, event | category | flops | bytes accessed | tf_op | source)
XLA Modules:
  0.0 902.2 jit_solution(1432756946718137325)
XLA Ops:
  0.0 1.4 fusion.key_ref
  1.4 20.0 %combine.3 = bf16[512,4096]{1,0:T(8,128)(2,1)} custom-call(s32[6,2,512]{2,1,0:T(2,128)} %fusion.key_ref, f32[6,2,512]{2,1,0:T(2,128)} %bitcast.21, bf16[6,4,320,4096]{3,2,1,0:T(8,128)(2,1)} %expert_ref.5, bf16[6,1,512,4096]{3,2,1,0:T(8,128)(2,1)} %res_ref.5), custom_call_target="tpu_custom_call" | custom-call | flops 10737418240 | bytes 18874368 | tf_op jit(solution)/shard_map/combine/pallas_call | solution.py:109
  21.4 1.5 collective-permute-start.5
  22.9 35.4 %combine.4 = (bf16[512,4096]{1,0:T(8,128)(2,1)}, bf16[512,4096]{1,0:T(8,128)(2,1)}) custom-call(s32[6,2,512]{2,1,0:T(2,128)} %fusion.key_ref, f32[6,2,512]{2,1,0:T(2,128)} %bitcast.22, bf16[6,4,320,4096]{3,2,1,0:T(8,128)(2,1)} %expert_ref.5, bf16[6,1,512,4096]{3,2,1,0:T(8,128)(2,1)} %res_ref.5), custom_call_target="tpu_custom_call" | custom-call | flops 21474836480 | bytes 37748736 | tf_op jit(solution)/shard_map/combine/pallas_call | solution.py:109
  58.3 0.1 collective-permute-start.4
  58.4 1.9 collective-permute-start.3
  60.3 50.5 %combine.5 = (bf16[512,4096]{1,0:T(8,128)(2,1)}, bf16[512,4096]{1,0:T(8,128)(2,1)}, bf16[512,4096]{1,0:T(8,128)(2,1)}) custom-call(s32[6,2,512]{2,1,0:T(2,128)} %fusion.key_ref, f32[6,2,512]{2,1,0:T(2,128)} %bitcast.23, bf16[6,4,320,4096]{3,2,1,0:T(8,128)(2,1)} %expert_ref.5, bf16[6,1,512,4096]{3,2,1,0:T(8,128)(2,1)} %res_ref.5), custom_call_target="tpu_custom_call" | custom-call | flops 32212254720 | bytes 56623104 | tf_op jit(solution)/shard_map/combine/pallas_call | solution.py:109
  110.9 1.5 collective-permute-start.1
  112.4 1.5 collective-permute-start
  113.9 33.3 %regroup.3.wq_hbm = bf16[8,4096,512]{2,1,0:T(8,128)(2,1)} custom-call(bf16[1,4096,32,128]{3,2,1,0:T(8,128)(2,1)} %wt_ref), custom_call_target="tpu_custom_call" | custom-call | flops 10000000000 | bytes 67108864 | tf_op jit(solution)/shard_map/regroup/pallas_call | solution.py:151
  147.2 33.3 %regroup.4.wk_hbm = bf16[8,4096,512]{2,1,0:T(8,128)(2,1)} custom-call(bf16[1,4096,32,128]{3,2,1,0:T(8,128)(2,1)} %wt_ref.1), custom_call_target="tpu_custom_call" | custom-call | flops 10000000000 | bytes 67108864 | tf_op jit(solution)/shard_map/regroup/pallas_call | solution.py:151
  180.5 33.3 %regroup.5.wv_hbm = bf16[8,4096,512]{2,1,0:T(8,128)(2,1)} custom-call(bf16[1,4096,32,128]{3,2,1,0:T(8,128)(2,1)} %wt_ref.2), custom_call_target="tpu_custom_call" | custom-call | flops 10000000000 | bytes 67108864 | tf_op jit(solution)/shard_map/regroup/pallas_call | solution.py:151
  213.9 0.0 collective-permute-done.5.y_hbm
  213.9 0.1 collective-permute-start.2
  213.9 112.6 %attention.6.refs_0_ = bf16[6,1,512,4096]{3,2,1,0:T(8,128)(2,1)} custom-call(f32[1,4096]{1,0:T(1,128)} %norm_ref.11, bf16[512,4096]{1,0:T(8,128)(2,1)} %collective-permute-done.5.y_hbm, bf16[8,4096,512]{2,1,0:T(8,128)(2,1)} %regroup.3.wq_hbm, bf16[8,4096,512]{2,1,0:T(8,128)(2,1)} %regroup.4.wk_hbm, bf16[8,4096,512]{2,1,0:T(8,128)(2,1)} %regroup.5.wv_hbm, ...), custom_call_target="tpu_custom_call" | custom-call | flops 68719476736 | bytes 134217728 | tf_op jit(solution)/shard_map/attention/pallas_call | solution.py:284
  326.5 0.0 collective-permute-done.4.y_hbm
  326.5 112.3 %attention.7.refs_0_ = bf16[6,1,512,4096]{3,2,1,0:T(8,128)(2,1)} custom-call(f32[1,4096]{1,0:T(1,128)} %norm_ref.11, bf16[512,4096]{1,0:T(8,128)(2,1)} %collective-permute-done.4.y_hbm, bf16[8,4096,512]{2,1,0:T(8,128)(2,1)} %regroup.3.wq_hbm, bf16[8,4096,512]{2,1,0:T(8,128)(2,1)} %regroup.4.wk_hbm, ...), custom_call_target="tpu_custom_call", output_to_operand_aliasing={{}: (6, {})} | custom-call | flops 68719476736 | bytes 134217728 | tf_op jit(solution)/shard_map/attention/pallas_call | solution.py:284
  438.9 0.0 collective-permute-done.3.y_hbm
  438.9 112.4 %attention.8.refs_0_ = bf16[6,1,512,4096]{3,2,1,0:T(8,128)(2,1)} custom-call(f32[1,4096]{1,0:T(1,128)} %norm_ref.11, bf16[512,4096]{1,0:T(8,128)(2,1)} %collective-permute-done.3.y_hbm, bf16[8,4096,512]{2,1,0:T(8,128)(2,1)} %regroup.3.wq_hbm, bf16[8,4096,512]{2,1,0:T(8,128)(2,1)} %regroup.4.wk_hbm, ...), custom_call_target="tpu_custom_call", output_to_operand_aliasing={{}: (6, {})} | custom-call | flops 68719476736 | bytes 134217728 | tf_op jit(solution)/shard_map/attention/pallas_call | solution.py:284
  551.2 13.4 %collective-permute-done.2.y_hbm = bf16[512,4096]{1,0:T(8,128)(2,1)} collective-permute-done((bf16[512,4096]{1,0:T(8,128)(2,1)}, bf16[512,4096]{1,0:T(8,128)(2,1)}, u32[]{:S(2)}, u32[]{:S(2)}) %collective-permute-start.2) | collective-permute-done | bytes 4194336 | tf_op jit(solution)/shard_map/ppermute | solution.py:335
  564.7 112.5 %attention.9.refs_0_ = bf16[6,1,512,4096]{3,2,1,0:T(8,128)(2,1)} custom-call(f32[1,4096]{1,0:T(1,128)} %norm_ref.11, bf16[512,4096]{1,0:T(8,128)(2,1)} %collective-permute-done.2.y_hbm, bf16[8,4096,512]{2,1,0:T(8,128)(2,1)} %regroup.3.wq_hbm, bf16[8,4096,512]{2,1,0:T(8,128)(2,1)} %regroup.4.wk_hbm, ...), custom_call_target="tpu_custom_call", output_to_operand_aliasing={{}: (6, {})} | custom-call | flops 68719476736 | bytes 134217728 | tf_op jit(solution)/shard_map/attention/pallas_call | solution.py:284
  677.2 0.0 collective-permute-done.1.y_hbm
  677.2 112.4 %attention.10.refs_0_ = bf16[6,1,512,4096]{3,2,1,0:T(8,128)(2,1)} custom-call(f32[1,4096]{1,0:T(1,128)} %norm_ref.11, bf16[512,4096]{1,0:T(8,128)(2,1)} %collective-permute-done.1.y_hbm, bf16[8,4096,512]{2,1,0:T(8,128)(2,1)} %regroup.3.wq_hbm, bf16[8,4096,512]{2,1,0:T(8,128)(2,1)} %regroup.4.wk_hbm, ...), custom_call_target="tpu_custom_call", output_to_operand_aliasing={{}: (6, {})} | custom-call | flops 68719476736 | bytes 134217728 | tf_op jit(solution)/shard_map/attention/pallas_call | solution.py:284
  789.6 0.0 collective-permute-done.y_hbm
  789.6 112.4 %attention.11 = bf16[6,1,512,4096]{3,2,1,0:T(8,128)(2,1)} custom-call(f32[1,4096]{1,0:T(1,128)} %norm_ref.11, bf16[512,4096]{1,0:T(8,128)(2,1)} %collective-permute-done.y_hbm, bf16[8,4096,512]{2,1,0:T(8,128)(2,1)} %regroup.3.wq_hbm, bf16[8,4096,512]{2,1,0:T(8,128)(2,1)} %regroup.4.wk_hbm, ...), custom_call_target="tpu_custom_call", output_to_operand_aliasing={{}: (6, {})} | custom-call | flops 68719476736 | bytes 134217728 | tf_op jit(solution)/shard_map/attention/pallas_call | solution.py:284
Async XLA Ops:
  21.4 192.5 %collective-permute-start.5 = (bf16[512,4096]{1,0:T(8,128)(2,1)}, bf16[512,4096]{1,0:T(8,128)(2,1)}, u32[]{:S(2)}, u32[]{:S(2)}) collective-permute-start(bf16[512,4096]{1,0:T(8,128)(2,1)} %combine.3), channel_id=1, source_target_pairs={{0,2},{2,4},{4,6},{6,0},{1,3},{3,5},{5,7},{7,1}} | collective-permute-start | bytes 12582920 | tf_op jit(solution)/shard_map/ppermute | solution.py:335
  58.3 268.2 %collective-permute-start.4 = (bf16[512,4096]{1,0:T(8,128)(2,1)}, bf16[512,4096]{1,0:T(8,128)(2,1)}, u32[]{:S(2)}, u32[]{:S(2)}) collective-permute-start(bf16[512,4096]{1,0:T(8,128)(2,1)} %get-tuple-element.31), channel_id=1, source_target_pairs={{0,2},{2,4},{4,6},{6,0},{1,3},{3,5},{5,7},{7,1}} | collective-permute-start | bytes 12582920 | tf_op jit(solution)/shard_map/ppermute | solution.py:335
  58.4 380.4 %collective-permute-start.3 = (bf16[512,4096]{1,0:T(8,128)(2,1)}, bf16[512,4096]{1,0:T(8,128)(2,1)}, u32[]{:S(2)}, u32[]{:S(2)}) collective-permute-start(bf16[512,4096]{1,0:T(8,128)(2,1)} %get-tuple-element.26), channel_id=1, source_target_pairs={{0,2},{2,4},{4,6},{6,0},{1,3},{3,5},{5,7},{7,1}} | collective-permute-start | bytes 12582920 | tf_op jit(solution)/shard_map/ppermute | solution.py:335
  110.9 566.3 %collective-permute-start.1 = (bf16[512,4096]{1,0:T(8,128)(2,1)}, bf16[512,4096]{1,0:T(8,128)(2,1)}, u32[]{:S(2)}, u32[]{:S(2)}) collective-permute-start(bf16[512,4096]{1,0:T(8,128)(2,1)} %get-tuple-element.29), channel_id=1, source_target_pairs={{0,2},{2,4},{4,6},{6,0},{1,3},{3,5},{5,7},{7,1}} | collective-permute-start | bytes 12582920 | tf_op jit(solution)/shard_map/ppermute | solution.py:335
  112.4 677.2 %collective-permute-start = (bf16[512,4096]{1,0:T(8,128)(2,1)}, bf16[512,4096]{1,0:T(8,128)(2,1)}, u32[]{:S(2)}, u32[]{:S(2)}) collective-permute-start(bf16[512,4096]{1,0:T(8,128)(2,1)} %get-tuple-element.28), channel_id=1, source_target_pairs={{0,2},{2,4},{4,6},{6,0},{1,3},{3,5},{5,7},{7,1}} | collective-permute-start | bytes 12582920 | tf_op jit(solution)/shard_map/ppermute | solution.py:335
  213.9 350.8 %collective-permute-start.2 = (bf16[512,4096]{1,0:T(8,128)(2,1)}, bf16[512,4096]{1,0:T(8,128)(2,1)}, u32[]{:S(2)}, u32[]{:S(2)}) collective-permute-start(bf16[512,4096]{1,0:T(8,128)(2,1)} %get-tuple-element.30), channel_id=1, source_target_pairs={{0,2},{2,4},{4,6},{6,0},{1,3},{3,5},{5,7},{7,1}} | collective-permute-start | bytes 12582920 | tf_op jit(solution)/shard_map/ppermute | solution.py:335

commit v4 on v3

--- a/solution.py
+++ b/solution.py
@@ -101,7 +101,7 @@
     tokens = residual.shape[2]
     depth = 2 * experts * src_slots
     count, tiles, base = len(micros), d_model // width, micros[0]
-    slots = 2 * count
+    slots = tiles * count
 
     def out_spec(at):
         return pl.BlockSpec((tokens, width), lambda m, n: (0, jnp.where(m < at, 0, jnp.where(m > at, tiles - 1, n))))
@@ -144,71 +144,88 @@
             out_ref[group, :, place * head_dim:(place + 1) * head_dim] = wide[pl.ds(head, rows, stride=sub), :].astype(out_ref.dtype)
 
 
-def regroup(weight, rows, width):
+def regroup(position, weight, rows, width):
     _, d_model, num_heads, head_dim = weight.shape
-    groups = num_heads * head_dim // width
+    heads = num_heads // 2
+    groups = heads * head_dim // width
     sub = 8
     return pl.pallas_call(
-        regroup_kernel,
+        lambda pos_ref, *refs: regroup_kernel(*refs),
         out_shape=jax.ShapeDtypeStruct((groups, d_model, width), weight.dtype),
-        grid=(d_model // rows,),
-        in_specs=[pl.BlockSpec((1, rows, num_heads, head_dim), lambda r: (0, r, 0, 0))],
-        out_specs=pl.BlockSpec((groups, rows, width), lambda r: (0, r, 0)),
-        scratch_shapes=[pltpu.VMEM((2, rows * sub, head_dim), jnp.float32)],
+        grid_spec=pltpu.PrefetchScalarGridSpec(
+            num_scalar_prefetch=1,
+            grid=(d_model // rows,),
+            in_specs=[pl.BlockSpec((1, rows, heads, head_dim), lambda r, pos: (0, r, pos[0], 0))],
+            out_specs=pl.BlockSpec((groups, rows, width), lambda r, pos: (0, r, 0)),
+            scratch_shapes=[pltpu.VMEM((2, rows * sub, head_dim), jnp.float32)],
+        ),
         compiler_params=pltpu.CompilerParams(vmem_limit_bytes=60 << 20),
-        cost_estimate=pl.CostEstimate(flops=10 ** 10, bytes_accessed=4 * d_model * num_heads * head_dim, transcendentals=0),
+        cost_estimate=pl.CostEstimate(flops=10 ** 10, bytes_accessed=2 * d_model * num_heads * head_dim, transcendentals=0),
         name='regroup',
-    )(weight)
-
-
-def attend(q_ref, k_ref, v_ref, head, part):
-    seq_len, head_dim = q_ref.shape[0], LANES
-    block = seq_len // 2
-    cols = slice(head * head_dim, (head + 1) * head_dim)
-    rows = slice(part * block, (part + 1) * block)
-    contract = (((1,), (1,)), ((), ()))
-    query = q_ref[rows, cols]
-    seen = lax.broadcasted_iota(jnp.int32, (block, block), 0) >= lax.broadcasted_iota(jnp.int32, (block, block), 1)
-    last = lax.dot_general(query, k_ref[rows, cols], contract, preferred_element_type=jnp.float32)
-    scores = jnp.where(seen, last, -jnp.inf)
-    if part:
-        early = lax.dot_general(query, k_ref[:block, cols], contract, preferred_element_type=jnp.float32)
-        scores = jnp.concatenate([early, scores], axis=1)
-    top = jnp.max(scores, axis=1, keepdims=True)
-    grown = jnp.exp2((scores - top) * ((head_dim ** -0.5) * LOG2E))
-    probs = (grown * (1.0 / jnp.sum(grown, axis=1, keepdims=True))).astype(jnp.bfloat16)
-    mixed = jnp.dot(probs, v_ref[:(part + 1) * block, cols], preferred_element_type=jnp.float32)
-    return rows, mixed.astype(jnp.bfloat16)
-
-
-def attention_kernel(norm_ref, y_hbm, wq_hbm, wk_hbm, wv_hbm, wo_hbm, *refs):
-    out_ref, y_ref, x_ref, attn_ref, wt_ref, wo_ref, *head_refs, y_sem, wt_sem, wo_sem = refs[-15:]
-    fresh, ready = head_refs[:3], head_refs[3:]
+    )(position, weight)
+
+
+def score(q_ref, k_ref, score_ref, head, part):
+    block = q_ref.shape[0] // 2
+    cols = slice(head * LANES, (head + 1) * LANES)
+    keys = (part + 1) * block
+    score_ref[:, :keys] = lax.dot_general(q_ref[part * block:keys, cols], k_ref[:keys, cols], (((1,), (1,)), ((), ())), preferred_element_type=jnp.float32)
+
+
+def causal_softmax(score_ref, prob_ref, part):
+    block = score_ref.shape[0]
+    strip = 32
+    keys = (part + 1) * block
+    row_pos = lax.broadcasted_iota(jnp.int32, (strip, LANES), 0)
+    col_pos = lax.broadcasted_iota(jnp.int32, (strip, LANES), 1)
+    for at in range(0, block, strip):
+        here = slice(at, at + strip)
+        diagonal = (part * block + at) // LANES * LANES
+        seen = row_pos + (part * block + at - diagonal) >= col_pos
+        last = jnp.where(seen, score_ref[here, diagonal:diagonal + LANES], -jnp.inf)
+        pieces = [score_ref[here, col:col + LANES] for col in range(0, diagonal, LANES)] + [last]
+        top = jnp.max(functools.reduce(jnp.maximum, pieces), axis=1, keepdims=True)
+        pieces = [jnp.exp2((piece - top) * ((LANES ** -0.5) * LOG2E)) for piece in pieces]
+        scale = 1.0 / jnp.sum(functools.reduce(jnp.add, pieces), axis=1, keepdims=True)
+        for which, piece in enumerate(pieces):
+            prob_ref[here, which * LANES:(which + 1) * LANES] = (piece * scale).astype(jnp.bfloat16)
+        if diagonal + LANES < keys:
+            prob_ref[here, diagonal + LANES:keys] = jnp.zeros((strip, keys - diagonal - LANES), jnp.bfloat16)
+
+
+def attention_kernel(norm_ref, y_hbm, wq_hbm, wk_hbm, wv_hbm, oq_hbm, ok_hbm, ov_hbm, wo_hbm, *refs):
+    out_ref, y_ref, x_ref, attn_ref, wt_ref, wo_ref, q_ref, k_ref, v_ref, *unit_refs, y_sem, wt_sem, wo_sem = refs[-28:]
+    score_refs, prob_refs = unit_refs[:8], unit_refs[8:]
     seq_len, d_model = y_ref.shape
-    depth = attn_ref.shape[1]
-    steps, _, width = wq_hbm.shape
+    own_groups, _, width = wq_hbm.shape
+    steps = 2 * own_groups
     tile = wo_ref.shape[2]
-    units = [(head, part) for head in range(width // LANES) for part in range(2)]
     step = pl.program_id(0)
-
-    def wt_copies(at):
-        return [pltpu.make_async_copy(hbm.at[at], wt_ref.at[at % 2, which], wt_sem.at[at % 2, which]) for which, hbm in enumerate((wq_hbm, wk_hbm, wv_hbm))]
+    me = lax.axis_index('ep')
+
+    def wt_copies(at, sources):
+        return [pltpu.make_async_copy(hbm.at[at % own_groups], wt_ref.at[at % 2, which], wt_sem.at[at % 2, which]) for which, hbm in enumerate(sources)]
+
+    def start_weights(at):
+        @pl.when(at // own_groups == me)
+        def _():
+            for copy in wt_copies(at, (wq_hbm, wk_hbm, wv_hbm)):
+                copy.start()
+
+        @pl.when(at // own_groups != me)
+        def _():
+            for copy in wt_copies(at, (oq_hbm, ok_hbm, ov_hbm)):
+                copy.start()
 
     def wo_copy(at):
         cols = pl.ds(pl.multiple_of(at * tile, tile), tile)
         return pltpu.make_async_copy(wo_hbm.at[:, cols], wo_ref.at[at % 2], wo_sem.at[at % 2])
 
-    def finish(at, proj):
-        y_tile = y_ref[:, pl.ds(pl.multiple_of(at * tile, tile), tile)]
-        rounded = proj.astype(jnp.bfloat16).astype(jnp.float32)
-        out_ref[0, 0] = (y_tile.astype(jnp.float32) + rounded).astype(out_ref.dtype)
-
     @pl.when(step == 0)
     def _():
         y_copy = pltpu.make_async_copy(y_hbm, y_ref, y_sem)
         y_copy.start()
-        for copy in wt_copies(0):
-            copy.start()
+        start_weights(step)
         y_copy.wait()
         strip = 32
 
@@ -220,45 +237,39 @@
             return carry
 
         lax.fori_loop(0, seq_len // strip, norm_strip, 0)
-        for ref in ready:
-            ref[...] = jnp.zeros_like(ref)
 
     @pl.when(step < steps)
     def _():
         @pl.when(step < steps - 1)
         def _():
-            for copy in wt_copies(step + 1):
-                copy.start()
+            start_weights(step + 1)
 
         @pl.when(step == steps - 1)
         def _():
             wo_copy(0).start()
 
-        for copy in wt_copies(step):
+        for copy in wt_copies(step, (wq_hbm, wk_hbm, wv_hbm)):
             copy.wait()
         slot = step % 2
-        base = jnp.where(step == 0, steps - 1, step - 1) * width
-        share = (len(units) + 2) // 3
-        for which in range(3):
-            fresh[which][...] = jnp.dot(x_ref[...], wt_ref[slot, which], preferred_element_type=jnp.float32).astype(jnp.bfloat16)
-            for head, part in units[which * share:(which + 1) * share]:
-                rows, mixed = attend(*ready, head, part)
-                attn_ref[rows, pl.ds(pl.multiple_of(base + head * LANES, LANES), LANES)] = mixed
-        for src_ref, dst_ref in zip(fresh, ready):
-            dst_ref[...] = src_ref[...]
-
-    @pl.when(step == steps)
-    def _():
-        wo_copy(1).start()
-        wo_copy(0).wait()
-        early = depth - width
-        proj = jnp.dot(attn_ref[:, :early], wo_ref[0, :early], preferred_element_type=jnp.float32)
-        for head, part in units:
-            rows, mixed = attend(*ready, head, part)
-            attn_ref[rows, early + head * LANES:early + (head + 1) * LANES] = mixed
-        finish(0, proj + jnp.dot(attn_ref[:, early:], wo_ref[0, early:], preferred_element_type=jnp.float32))
-
-    @pl.when(step > steps)
+
+        def emit(which, dst_ref):
+            dst_ref[...] = jnp.dot(x_ref[...], wt_ref[slot, which], preferred_element_type=jnp.float32).astype(jnp.bfloat16)
+
+        block = seq_len // 2
+        units = [(head, part) for head in range(width // LANES) for part in range(2)]
+        emit(0, q_ref)
+        emit(1, k_ref)
+        for at, (head, part) in enumerate(units):
+            score(q_ref, k_ref, score_refs[at], head, part)
+        emit(2, v_ref)
+        for at, (head, part) in enumerate(units):
+            causal_softmax(score_refs[at], prob_refs[at], part)
+        for at, (head, part) in enumerate(units):
+            keys = (part + 1) * block
+            mixed = jnp.dot(prob_refs[at][:, :keys], v_ref[:keys, head * LANES:(head + 1) * LANES], preferred_element_type=jnp.float32)
+            attn_ref[part * block:keys, pl.ds(pl.multiple_of(step * width + head * LANES, LANES), LANES)] = mixed.astype(jnp.bfloat16)
+
+    @pl.when(step >= steps)
     def _():
         at = step - steps
 
@@ -267,12 +278,15 @@
             wo_copy(at + 1).start()
 
         wo_copy(at).wait()
-        finish(at, jnp.dot(attn_ref[...], wo_ref[at % 2], preferred_element_type=jnp.float32))
+        proj = jnp.dot(attn_ref[...], wo_ref[at % 2], preferred_element_type=jnp.float32).astype(jnp.bfloat16)
+        y_tile = y_ref[:, pl.ds(pl.multiple_of(at * tile, tile), tile)]
+        out_ref[0, 0] = (y_tile.astype(jnp.float32) + proj.astype(jnp.float32)).astype(out_ref.dtype)
 
 
 def attention(micro, arrived, norm_w, weights, w_out, result, out_shape, tile):
     seq_len, d_model = arrived.shape
     steps, _, width = weights[0].shape
+    steps = 2 * steps
     depth = steps * width
     hbm = pl.BlockSpec(memory_space=pl.ANY)
     operands = [norm_w, arrived, *weights, w_out]
@@ -293,7 +307,9 @@
             pltpu.VMEM((seq_len, depth), jnp.bfloat16),
             pltpu.VMEM((2, 3, d_model, width), jnp.bfloat16),
             pltpu.VMEM((2, depth, tile), jnp.bfloat16),
-            *[head_group] * 6,
+            *[head_group] * 3,
+            *[pltpu.VMEM((seq_len // 2, seq_len), jnp.float32)] * 8,
+            *[pltpu.VMEM((seq_len // 2, seq_len), jnp.bfloat16)] * 8,
             pltpu.SemaphoreType.DMA,
             pltpu.SemaphoreType.DMA((2, 3)),
             pltpu.SemaphoreType.DMA((2,)),
@@ -309,6 +325,7 @@
     stages = mesh.shape['pp']
     group_size = mesh.shape['ep']
     send_next = [(src, (src + 1) % stages) for src in range(stages)]
+    swap_pair = [(src, (src + 1) % group_size) for src in range(group_size)]
     tok_spec = P('pp', 'ep', None, None)
     wt_spec = P('pp', None, None, None)
 
@@ -324,6 +341,17 @@
         keys = jnp.swapaxes(keys, 1, 2)
         gates = jnp.swapaxes(gate_vals[:, 0], 1, 2)
 
+        halves = []
+        for wt in (w_query, w_key, w_value):
+            if halves:
+                wt = lax.optimization_barrier((wt, halves[-1]))[0]
+            halves.append(regroup(position[None], wt, 256, 512))
+        crossed = []
+        for half in halves:
+            crossed.append(lax.ppermute(half, 'ep', swap_pair))
+        weights = [*halves, *crossed]
+
+        keys = lax.optimization_barrier((keys, halves[-1]))[0]
         arrived = []
         combined = []
         for call_id, micros in enumerate(((0,), (1, 2), (3, 4, 5))):
@@ -333,13 +361,11 @@
             combined.extend(rows)
             for micro, row in zip(micros, rows):
                 arrived.append(lax.ppermute(row, 'pp', send_next))
-        raw = lax.optimization_barrier((w_query, w_key, w_value, combined[-1]))[:3]
-        weights = [regroup(wt, 256, 512) for wt in raw]
 
         flat_out = w_out[0].reshape(-1, d_model)
         result = None
         for micro in range(num_micro):
-            rows = arrived[micro]
+            rows = lax.optimization_barrier((arrived[0], combined[-1]))[0] if micro == 0 else arrived[micro]
             if micro:
                 rows, result = lax.optimization_barrier((rows, result))
             result = attention(micro, rows, norm_w, weights, flat_out, result, residual.shape, 512)

time: 913 us -> 990 us (1.084)
  waiting for transfers between devices: 13.4 us -> 184 us
  Pallas kernels: 880 us -> 788 us
    ppermute x6, waiting for transfers between devices: 13.4 us -> 184 us  [device_step(): arrived.append(lax.ppermute(row, 'pp', send_next))]
    pallas_call x6, Pallas kernels: 675 us -> 559 us  [attention(): pl.pallas_call(attention_kernel, out_shape=jax.ShapeDtypeStruct(out_shape...]
    pallas_call x3, Pallas kernels: 106 us -> 168 us  [combine(): pl.pallas_call(functools.partial(combine_kernel, micros), out_shape=[jax....]
    pallas_call x3, Pallas kernels: 100 us -> 61.5 us  [regroup(): pl.pallas_call(lambda pos_ref, *refs: regroup_kernel(*refs), out_shape=ja...]
  transfers between devices with their start and end apart: 6 -> 9, of which waited for: 1 -> 2; matrix products, arithmetic and copies ran while one was open for 0% -> 0% of each run, Pallas kernels for 83% -> 65%
where the time goes in v4:
time: 990 us; the launch traced here: 980 us
  Pallas kernels  788 us (80%)
  waiting for transfers between devices  184 us (19%)
    pallas_call x6, Pallas kernels, attention(): pl.pallas_call(attention_kernel, out_shape=jax.ShapeDtypeStruct(out_shape...  559 us
    ppermute x6, waiting for transfers between devices, device_step(): arrived.append(lax.ppermute(row, 'pp', send_next))  184 us
    pallas_call x3, Pallas kernels, combine(): pl.pallas_call(functools.partial(combine_kernel, micros), out_shape=[jax....  168 us
    pallas_call x3, Pallas kernels, regroup(): pl.pallas_call(lambda pos_ref, *refs: regroup_kernel(*refs), out_shape=ja...  61.5 us
  transfers between devices with their start and end apart: 9, of which 2 were waited for; matrix products, arithmetic and copies ran while one was open for 0% of the time, Pallas kernels for 65%

profile of v4, /device:TPU:4, one launch (start us, length us, event | category | flops | bytes accessed | tf_op | source)
XLA Modules:
  0.0 979.9 jit_solution(13518236745494211128)
XLA Ops:
  0.0 20.5 %regroup.3.wq_hbm = bf16[4,4096,512]{2,1,0:T(8,128)(2,1)} custom-call(s32[1]{0:T(128)} %bitcast.4.pos_ref, bf16[1,4096,32,128]{3,2,1,0:T(8,128)(2,1)} %refs_0_.1), custom_call_target="tpu_custom_call" | custom-call | flops 10000000000 | bytes 33554432 | tf_op jit(solution)/shard_map/regroup/pallas_call | solution.py:152
  20.5 20.5 %regroup.4.wk_hbm = bf16[4,4096,512]{2,1,0:T(8,128)(2,1)} custom-call(s32[1]{0:T(128)} %bitcast.4.pos_ref, bf16[1,4096,32,128]{3,2,1,0:T(8,128)(2,1)} %refs_0_.2), custom_call_target="tpu_custom_call" | custom-call | flops 10000000000 | bytes 33554432 | tf_op jit(solution)/shard_map/regroup/pallas_call | solution.py:152
  41.0 0.0 copy-start
  41.0 0.0 copy-start.1
  41.0 20.5 %regroup.5.wv_hbm = bf16[4,4096,512]{2,1,0:T(8,128)(2,1)} custom-call(s32[1]{0:T(128)} %bitcast.4.pos_ref, bf16[1,4096,32,128]{3,2,1,0:T(8,128)(2,1)} %refs_0_.3), custom_call_target="tpu_custom_call" | custom-call | flops 10000000000 | bytes 33554432 | tf_op jit(solution)/shard_map/regroup/pallas_call | solution.py:152
  61.5 0.0 collective-permute-start.8
  61.5 0.5 collective-permute-start.7
  62.0 0.0 collective-permute-start.6
  62.0 0.0 copy-done
  62.0 0.0 copy-done.1
  62.0 0.7 fusion.key_ref
  62.7 87.0 %combine.3 = bf16[512,4096]{1,0:T(8,128)(2,1)} custom-call(s32[6,2,512]{2,1,0:T(2,128)} %fusion.key_ref, f32[6,2,512]{2,1,0:T(2,128)} %bitcast.22, bf16[6,4,320,4096]{3,2,1,0:T(8,128)(2,1)} %expert_ref.5, bf16[6,1,512,4096]{3,2,1,0:T(8,128)(2,1)} %res_ref.5), custom_call_target="tpu_custom_call" | custom-call | flops 10737418240 | bytes 18874368 | tf_op jit(solution)/shard_map/combine/pallas_call | solution.py:109
  149.7 1.5 collective-permute-start.5
  151.2 32.6 %combine.4 = (bf16[512,4096]{1,0:T(8,128)(2,1)}, bf16[512,4096]{1,0:T(8,128)(2,1)}) custom-call(s32[6,2,512]{2,1,0:T(2,128)} %fusion.key_ref, f32[6,2,512]{2,1,0:T(2,128)} %bitcast.23, bf16[6,4,320,4096]{3,2,1,0:T(8,128)(2,1)} %expert_ref.5, bf16[6,1,512,4096]{3,2,1,0:T(8,128)(2,1)} %res_ref.5), custom_call_target="tpu_custom_call" | custom-call | flops 21474836480 | bytes 37748736 | tf_op jit(solution)/shard_map/combine/pallas_call | solution.py:109
  183.8 0.1 collective-permute-start.3
  183.9 48.2 %combine.5 = (bf16[512,4096]{1,0:T(8,128)(2,1)}, bf16[512,4096]{1,0:T(8,128)(2,1)}, bf16[512,4096]{1,0:T(8,128)(2,1)}) custom-call(s32[6,2,512]{2,1,0:T(2,128)} %fusion.key_ref, f32[6,2,512]{2,1,0:T(2,128)} %bitcast.24, bf16[6,4,320,4096]{3,2,1,0:T(8,128)(2,1)} %expert_ref.5, bf16[6,1,512,4096]{3,2,1,0:T(8,128)(2,1)} %res_ref.5), custom_call_target="tpu_custom_call" | custom-call | flops 32212254720 | bytes 56623104 | tf_op jit(solution)/shard_map/combine/pallas_call | solution.py:109
  232.1 12.2 %collective-permute-done.5.y_hbm = bf16[512,4096]{1,0:T(8,128)(2,1)} collective-permute-done((bf16[512,4096]{1,0:T(8,128)(2,1)}, bf16[512,4096]{1,0:T(8,128)(2,1)}, u32[]{:S(2)}, u32[]{:S(2)}) %collective-permute-start.5) | collective-permute-done | bytes 4194336 | tf_op jit(solution)/shard_map/ppermute | solution.py:363
  244.3 0.6 collective-permute-start
  244.9 0.0 collective-permute-done.8.ov_hbm
  244.9 0.9 collective-permute-start.4
  245.8 0.0 collective-permute-done.7.ok_hbm
  245.9 1.1 collective-permute-start.1
  246.9 0.0 collective-permute-done.6.oq_hbm
  246.9 2.4 collective-permute-start.2
  249.3 93.1 %attention.6.refs_0_ = bf16[6,1,512,4096]{3,2,1,0:T(8,128)(2,1)} custom-call(f32[1,4096]{1,0:T(1,128)} %norm_ref.11, bf16[512,4096]{1,0:T(8,128)(2,1)} %collective-permute-done.5.y_hbm, bf16[4,4096,512]{2,1,0:T(8,128)(2,1)} %regroup.3.wq_hbm, bf16[4,4096,512]{2,1,0:T(8,128)(2,1)} %regroup.4.wk_hbm, bf16[4,4096,512]{2,1,0:T(8,128)(2,1)} %regroup.5.wv_hbm, ...), custom_call_target="tpu_custom_call" | custom-call | flops 68719476736 | bytes 134217728 | tf_op jit(solution)/shard_map/attention/pallas_call | solution.py:298
  342.4 171.6 %collective-permute-done.4.y_hbm = bf16[512,4096]{1,0:T(8,128)(2,1)} collective-permute-done((bf16[512,4096]{1,0:T(8,128)(2,1)}, bf16[512,4096]{1,0:T(8,128)(2,1)}, u32[]{:S(2)}, u32[]{:S(2)}) %collective-permute-start.4) | collective-permute-done | bytes 4194336 | tf_op jit(solution)/shard_map/ppermute | solution.py:363
  514.0 93.3 %attention.7.refs_0_ = bf16[6,1,512,4096]{3,2,1,0:T(8,128)(2,1)} custom-call(f32[1,4096]{1,0:T(1,128)} %norm_ref.11, bf16[512,4096]{1,0:T(8,128)(2,1)} %collective-permute-done.4.y_hbm, bf16[4,4096,512]{2,1,0:T(8,128)(2,1)} %regroup.3.wq_hbm, bf16[4,4096,512]{2,1,0:T(8,128)(2,1)} %regroup.4.wk_hbm, ...), custom_call_target="tpu_custom_call", output_to_operand_aliasing={{}: (9, {})} | custom-call | flops 68719476736 | bytes 134217728 | tf_op jit(solution)/shard_map/attention/pallas_call | solution.py:298
  607.3 0.0 collective-permute-done.3.y_hbm
  607.3 93.1 %attention.8.refs_0_ = bf16[6,1,512,4096]{3,2,1,0:T(8,128)(2,1)} custom-call(f32[1,4096]{1,0:T(1,128)} %norm_ref.11, bf16[512,4096]{1,0:T(8,128)(2,1)} %collective-permute-done.3.y_hbm, bf16[4,4096,512]{2,1,0:T(8,128)(2,1)} %regroup.3.wq_hbm, bf16[4,4096,512]{2,1,0:T(8,128)(2,1)} %regroup.4.wk_hbm, ...), custom_call_target="tpu_custom_call", output_to_operand_aliasing={{}: (9, {})} | custom-call | flops 68719476736 | bytes 134217728 | tf_op jit(solution)/shard_map/attention/pallas_call | solution.py:298
  700.4 0.0 collective-permute-done.2.y_hbm
  700.4 93.0 %attention.9.refs_0_ = bf16[6,1,512,4096]{3,2,1,0:T(8,128)(2,1)} custom-call(f32[1,4096]{1,0:T(1,128)} %norm_ref.11, bf16[512,4096]{1,0:T(8,128)(2,1)} %collective-permute-done.2.y_hbm, bf16[4,4096,512]{2,1,0:T(8,128)(2,1)} %regroup.3.wq_hbm, bf16[4,4096,512]{2,1,0:T(8,128)(2,1)} %regroup.4.wk_hbm, ...), custom_call_target="tpu_custom_call", output_to_operand_aliasing={{}: (9, {})} | custom-call | flops 68719476736 | bytes 134217728 | tf_op jit(solution)/shard_map/attention/pallas_call | solution.py:298
  793.4 0.0 collective-permute-done.1.y_hbm
  793.4 93.1 %attention.10.refs_0_ = bf16[6,1,512,4096]{3,2,1,0:T(8,128)(2,1)} custom-call(f32[1,4096]{1,0:T(1,128)} %norm_ref.11, bf16[512,4096]{1,0:T(8,128)(2,1)} %collective-permute-done.1.y_hbm, bf16[4,4096,512]{2,1,0:T(8,128)(2,1)} %regroup.3.wq_hbm, bf16[4,4096,512]{2,1,0:T(8,128)(2,1)} %regroup.4.wk_hbm, ...), custom_call_target="tpu_custom_call", output_to_operand_aliasing={{}: (9, {})} | custom-call | flops 68719476736 | bytes 134217728 | tf_op jit(solution)/shard_map/attention/pallas_call | solution.py:298
  886.5 0.0 collective-permute-done.y_hbm
  886.5 93.1 %attention.11 = bf16[6,1,512,4096]{3,2,1,0:T(8,128)(2,1)} custom-call(f32[1,4096]{1,0:T(1,128)} %norm_ref.11, bf16[512,4096]{1,0:T(8,128)(2,1)} %collective-permute-done.y_hbm, bf16[4,4096,512]{2,1,0:T(8,128)(2,1)} %regroup.3.wq_hbm, bf16[4,4096,512]{2,1,0:T(8,128)(2,1)} %regroup.4.wk_hbm, ...), custom_call_target="tpu_custom_call", output_to_operand_aliasing={{}: (9, {})} | custom-call | flops 68719476736 | bytes 134217728 | tf_op jit(solution)/shard_map/attention/pallas_call | solution.py:298
Async XLA Ops:
  41.0 21.0 %copy-start = (s32[6,1,512,2]{2,3,1,0:T(2,128)S(1)}, s32[6,1,512,2]{2,3,1,0:T(2,128)}, u32[]{:S(2)}) copy-start(s32[6,1,512,2]{2,3,1,0:T(2,128)} %param.12) | copy-start | bytes 73732
  41.0 21.0 %copy-start.1 = (s32[6,1,512,2]{2,3,1,0:T(2,128)S(1)}, s32[6,1,512,2]{2,3,1,0:T(2,128)}, u32[]{:S(2)}) copy-start(s32[6,1,512,2]{2,3,1,0:T(2,128)} %param.11) | copy-start | bytes 73732
  61.5 183.5 %collective-permute-start.8 = (bf16[4,4096,512]{2,1,0:T(8,128)(2,1)}, bf16[4,4096,512]{2,1,0:T(8,128)(2,1)}, u32[]{:S(2)}, u32[]{:S(2)}) collective-permute-start(bf16[4,4096,512]{2,1,0:T(8,128)(2,1)} %regroup.5.wv_hbm), channel_id=1, source_target_pairs={{0,1},{1,0},{2,3},{3,2},{4,5},{5,4},{6,7},{7,6}} | collective-permute-start | bytes 50331656 | tf_op jit(solution)/shard_map/ppermute | solution.py:351
  61.5 184.4 %collective-permute-start.7 = (bf16[4,4096,512]{2,1,0:T(8,128)(2,1)}, bf16[4,4096,512]{2,1,0:T(8,128)(2,1)}, u32[]{:S(2)}, u32[]{:S(2)}) collective-permute-start(bf16[4,4096,512]{2,1,0:T(8,128)(2,1)} %regroup.4.wk_hbm), channel_id=1, source_target_pairs={{0,1},{1,0},{2,3},{3,2},{4,5},{5,4},{6,7},{7,6}} | collective-permute-start | bytes 50331656 | tf_op jit(solution)/shard_map/ppermute | solution.py:351
  62.0 184.9 %collective-permute-start.6 = (bf16[4,4096,512]{2,1,0:T(8,128)(2,1)}, bf16[4,4096,512]{2,1,0:T(8,128)(2,1)}, u32[]{:S(2)}, u32[]{:S(2)}) collective-permute-start(bf16[4,4096,512]{2,1,0:T(8,128)(2,1)} %regroup.3.wq_hbm), channel_id=1, source_target_pairs={{0,1},{1,0},{2,3},{3,2},{4,5},{5,4},{6,7},{7,6}} | collective-permute-start | bytes 50331656 | tf_op jit(solution)/shard_map/ppermute | solution.py:351
  149.7 94.7 %collective-permute-start.5 = (bf16[512,4096]{1,0:T(8,128)(2,1)}, bf16[512,4096]{1,0:T(8,128)(2,1)}, u32[]{:S(2)}, u32[]{:S(2)}) collective-permute-start(bf16[512,4096]{1,0:T(8,128)(2,1)} %combine.3), channel_id=1, source_target_pairs={{0,2},{2,4},{4,6},{6,0},{1,3},{3,5},{5,7},{7,1}} | collective-permute-start | bytes 12582920 | tf_op jit(solution)/shard_map/ppermute | solution.py:363
  183.8 423.5 %collective-permute-start.3 = (bf16[512,4096]{1,0:T(8,128)(2,1)}, bf16[512,4096]{1,0:T(8,128)(2,1)}, u32[]{:S(2)}, u32[]{:S(2)}) collective-permute-start(bf16[512,4096]{1,0:T(8,128)(2,1)} %get-tuple-element.30), channel_id=1, source_target_pairs={{0,2},{2,4},{4,6},{6,0},{1,3},{3,5},{5,7},{7,1}} | collective-permute-start | bytes 12582920 | tf_op jit(solution)/shard_map/ppermute | solution.py:363
  244.3 642.2 %collective-permute-start = (bf16[512,4096]{1,0:T(8,128)(2,1)}, bf16[512,4096]{1,0:T(8,128)(2,1)}, u32[]{:S(2)}, u32[]{:S(2)}) collective-permute-start(bf16[512,4096]{1,0:T(8,128)(2,1)} %get-tuple-element.32), channel_id=1, source_target_pairs={{0,2},{2,4},{4,6},{6,0},{1,3},{3,5},{5,7},{7,1}} | collective-permute-start | bytes 12582920 | tf_op jit(solution)/shard_map/ppermute | solution.py:363
  244.9 269.1 %collective-permute-start.4 = (bf16[512,4096]{1,0:T(8,128)(2,1)}, bf16[512,4096]{1,0:T(8,128)(2,1)}, u32[]{:S(2)}, u32[]{:S(2)}) collective-permute-start(bf16[512,4096]{1,0:T(8,128)(2,1)} %get-tuple-element.35), channel_id=1, source_target_pairs={{0,2},{2,4},{4,6},{6,0},{1,3},{3,5},{5,7},{7,1}} | collective-permute-start | bytes 12582920 | tf_op jit(solution)/shard_map/ppermute | solution.py:363
  245.9 547.6 %collective-permute-start.1 = (bf16[512,4096]{1,0:T(8,128)(2,1)}, bf16[512,4096]{1,0:T(8,128)(2,1)}, u32[]{:S(2)}, u32[]{:S(2)}) collective-permute-start(bf16[512,4096]{1,0:T(8,128)(2,1)} %get-tuple-element.33), channel_id=1, source_target_pairs={{0,2},{2,4},{4,6},{6,0},{1,3},{3,5},{5,7},{7,1}} | collective-permute-start | bytes 12582920 | tf_op jit(solution)/shard_map/ppermute | solution.py:363
  246.9 453.5 %collective-permute-start.2 = (bf16[512,4096]{1,0:T(8,128)(2,1)}, bf16[512,4096]{1,0:T(8,128)(2,1)}, u32[]{:S(2)}, u32[]{:S(2)}) collective-permute-start(bf16[512,4096]{1,0:T(8,128)(2,1)} %get-tuple-element.34), channel_id=1, source_target_pairs={{0,2},{2,4},{4,6},{6,0},{1,3},{3,5},{5,7},{7,1}} | collective-permute-start | bytes 12582920 | tf_op jit(solution)/shard_map/ppermute | solution.py:363

commit v5 on v4

--- a/solution.py
+++ b/solution.py
@@ -147,6 +147,8 @@
 def regroup(position, weight, rows, width):
     _, d_model, num_heads, head_dim = weight.shape
     heads = num_heads // 2
+    if position is None:
+        heads, position = num_heads, jnp.zeros((1,), jnp.int32)
     groups = heads * head_dim // width
     sub = 8
     return pl.pallas_call(
@@ -193,7 +195,7 @@
             prob_ref[here, diagonal + LANES:keys] = jnp.zeros((strip, keys - diagonal - LANES), jnp.bfloat16)
 
 
-def attention_kernel(norm_ref, y_hbm, wq_hbm, wk_hbm, wv_hbm, oq_hbm, ok_hbm, ov_hbm, wo_hbm, *refs):
+def attention_kernel(norm_ref, y_hbm, wq_hbm, wk_hbm, oq_hbm, ok_hbm, wv_hbm, wo_hbm, *refs):
     out_ref, y_ref, x_ref, attn_ref, wt_ref, wo_ref, q_ref, k_ref, v_ref, *unit_refs, y_sem, wt_sem, wo_sem = refs[-28:]
     score_refs, prob_refs = unit_refs[:8], unit_refs[8:]
     seq_len, d_model = y_ref.shape
@@ -203,18 +205,19 @@
     step = pl.program_id(0)
     me = lax.axis_index('ep')
 
-    def wt_copies(at, sources):
-        return [pltpu.make_async_copy(hbm.at[at % own_groups], wt_ref.at[at % 2, which], wt_sem.at[at % 2, which]) for which, hbm in enumerate(sources)]
+    def wt_copies(at, query_hbm, key_hbm):
+        sources = (query_hbm.at[at % own_groups], key_hbm.at[at % own_groups], wv_hbm.at[at])
+        return [pltpu.make_async_copy(src, wt_ref.at[at % 2, which], wt_sem.at[at % 2, which]) for which, src in enumerate(sources)]
 
     def start_weights(at):
         @pl.when(at // own_groups == me)
         def _():
-            for copy in wt_copies(at, (wq_hbm, wk_hbm, wv_hbm)):
+            for copy in wt_copies(at, wq_hbm, wk_hbm):
                 copy.start()
 
         @pl.when(at // own_groups != me)
         def _():
-            for copy in wt_copies(at, (oq_hbm, ok_hbm, ov_hbm)):
+            for copy in wt_copies(at, oq_hbm, ok_hbm):
                 copy.start()
 
     def wo_copy(at):
@@ -248,7 +251,7 @@
         def _():
             wo_copy(0).start()
 
-        for copy in wt_copies(step, (wq_hbm, wk_hbm, wv_hbm)):
+        for copy in wt_copies(step, wq_hbm, wk_hbm):
             copy.wait()
         slot = step % 2
 
@@ -341,19 +344,9 @@
         keys = jnp.swapaxes(keys, 1, 2)
         gates = jnp.swapaxes(gate_vals[:, 0], 1, 2)
 
-        halves = []
-        for wt in (w_query, w_key, w_value):
-            if halves:
-                wt = lax.optimization_barrier((wt, halves[-1]))[0]
-            halves.append(regroup(position[None], wt, 256, 512))
-        crossed = []
-        for half in halves:
-            crossed.append(lax.ppermute(half, 'ep', swap_pair))
-        weights = [*halves, *crossed]
-
-        keys = lax.optimization_barrier((keys, halves[-1]))[0]
         arrived = []
         combined = []
+        weights = []
         for call_id, micros in enumerate(((0,), (1, 2), (3, 4, 5))):
             if combined:
                 keys = lax.optimization_barrier((keys, combined[-1]))[0]
@@ -361,6 +354,18 @@
             combined.extend(rows)
             for micro, row in zip(micros, rows):
                 arrived.append(lax.ppermute(row, 'pp', send_next))
+            if call_id == 0:
+                before = combined[-1]
+                for wt in (w_query, w_key):
+                    wt = lax.optimization_barrier((wt, before))[0]
+                    before = regroup(position[None], wt, 256, 512)
+                    weights.append(before)
+                value_in = lax.optimization_barrier((w_value, before))[0]
+                value_wt = regroup(None, value_in, 256, 512)
+                for which in range(2):
+                    weights.append(lax.ppermute(weights[which], 'ep', swap_pair))
+                weights.append(value_wt)
+                keys = lax.optimization_barrier((keys, value_wt))[0]
 
         flat_out = w_out[0].reshape(-1, d_model)
         result = None

time: 990 us -> 893 us (0.902)
  waiting for transfers between devices: 184 us -> 130 us
  Pallas kernels: 788 us -> 743 us
    pallas_call x3, Pallas kernels: 168 us -> 110 us  [combine(): pl.pallas_call(functools.partial(combine_kernel, micros), out_shape=[jax....]
    ppermute x6, waiting for transfers between devices: 184 us -> 130 us  [device_step(): arrived.append(lax.ppermute(row, 'pp', send_next))]
    pallas_call x3, Pallas kernels: 61.5 us -> 74.3 us  [regroup(): pl.pallas_call(lambda pos_ref, *refs: regroup_kernel(*refs), out_shape=ja...]
  transfers between devices with their start and end apart: 9 -> 8, of which waited for: 2 -> 1; matrix products, arithmetic and copies ran while one was open for 0% -> 0% of each run, Pallas kernels for 65% -> 67%
where the time goes in v5:
time: 893 us; the launch traced here: 883 us
  Pallas kernels  743 us (83%)
  waiting for transfers between devices  130 us (15%)
    pallas_call x6, Pallas kernels, attention(): pl.pallas_call(attention_kernel, out_shape=jax.ShapeDtypeStruct(out_shape...  559 us
    ppermute x6, waiting for transfers between devices, device_step(): arrived.append(lax.ppermute(row, 'pp', send_next))  130 us
    pallas_call x3, Pallas kernels, combine(): pl.pallas_call(functools.partial(combine_kernel, micros), out_shape=[jax....  110 us
    pallas_call x3, Pallas kernels, regroup(): pl.pallas_call(lambda pos_ref, *refs: regroup_kernel(*refs), out_shape=ja...  74.3 us
  transfers between devices with their start and end apart: 8, of which 1 were waited for; matrix products, arithmetic and copies ran while one was open for 0% of the time, Pallas kernels for 67%

profile of v5, /device:TPU:4, one launch (start us, length us, event | category | flops | bytes accessed | tf_op | source)
XLA Modules:
  0.0 883.0 jit_solution(11059716556865238268)
XLA Ops:
  0.0 1.4 fusion.key_ref
  1.4 17.3 %combine.3 = bf16[512,4096]{1,0:T(8,128)(2,1)} custom-call(s32[6,2,512]{2,1,0:T(2,128)} %fusion.key_ref, f32[6,2,512]{2,1,0:T(2,128)} %bitcast.22, bf16[6,4,320,4096]{3,2,1,0:T(8,128)(2,1)} %expert_ref.5, bf16[6,1,512,4096]{3,2,1,0:T(8,128)(2,1)} %res_ref.5), custom_call_target="tpu_custom_call" | custom-call | flops 10737418240 | bytes 18874368 | tf_op jit(solution)/shard_map/combine/pallas_call | solution.py:109
  18.7 20.5 %regroup.3.wq_hbm = bf16[4,4096,512]{2,1,0:T(8,128)(2,1)} custom-call(s32[1]{0:T(128)} %bitcast.4.pos_ref, bf16[1,4096,32,128]{3,2,1,0:T(8,128)(2,1)} %refs_0_), custom_call_target="tpu_custom_call" | custom-call | flops 10000000000 | bytes 33554432 | tf_op jit(solution)/shard_map/regroup/pallas_call | solution.py:154
  39.2 20.5 %regroup.4.wk_hbm = bf16[4,4096,512]{2,1,0:T(8,128)(2,1)} custom-call(s32[1]{0:T(128)} %bitcast.4.pos_ref, bf16[1,4096,32,128]{3,2,1,0:T(8,128)(2,1)} %refs_0_.1), custom_call_target="tpu_custom_call" | custom-call | flops 10000000000 | bytes 33554432 | tf_op jit(solution)/shard_map/regroup/pallas_call | solution.py:154
  59.7 0.1 collective-permute-start.7
  59.8 0.4 collective-permute-start.6
  60.2 1.5 collective-permute-start.5
  61.7 33.3 %regroup.5.wv_hbm = bf16[8,4096,512]{2,1,0:T(8,128)(2,1)} custom-call(s32[1]{0:T(128)} %constant.28.clone.1.pos_ref, bf16[1,4096,32,128]{3,2,1,0:T(8,128)(2,1)} %refs_0_.2), custom_call_target="tpu_custom_call" | custom-call | flops 10000000000 | bytes 33554432 | tf_op jit(solution)/shard_map/regroup/pallas_call | solution.py:154
  95.0 44.2 %combine.4 = (bf16[512,4096]{1,0:T(8,128)(2,1)}, bf16[512,4096]{1,0:T(8,128)(2,1)}) custom-call(s32[6,2,512]{2,1,0:T(2,128)} %fusion.key_ref, f32[6,2,512]{2,1,0:T(2,128)} %bitcast.23, bf16[6,4,320,4096]{3,2,1,0:T(8,128)(2,1)} %expert_ref.5, bf16[6,1,512,4096]{3,2,1,0:T(8,128)(2,1)} %res_ref.5), custom_call_target="tpu_custom_call" | custom-call | flops 21474836480 | bytes 37748736 | tf_op jit(solution)/shard_map/combine/pallas_call | solution.py:109
  139.2 1.5 collective-permute-start.4
  140.7 0.0 collective-permute-start.3
  140.8 48.2 %combine.5 = (bf16[512,4096]{1,0:T(8,128)(2,1)}, bf16[512,4096]{1,0:T(8,128)(2,1)}, bf16[512,4096]{1,0:T(8,128)(2,1)}) custom-call(s32[6,2,512]{2,1,0:T(2,128)} %fusion.key_ref, f32[6,2,512]{2,1,0:T(2,128)} %bitcast.24, bf16[6,4,320,4096]{3,2,1,0:T(8,128)(2,1)} %expert_ref.5, bf16[6,1,512,4096]{3,2,1,0:T(8,128)(2,1)} %res_ref.5), custom_call_target="tpu_custom_call" | custom-call | flops 32212254720 | bytes 56623104 | tf_op jit(solution)/shard_map/combine/pallas_call | solution.py:109
  189.0 0.0 collective-permute-done.5.y_hbm
  189.0 2.0 collective-permute-start
  191.0 0.0 collective-permute-done.7.ok_hbm
  191.0 1.5 collective-permute-start.1
  192.5 0.0 collective-permute-done.6.oq_hbm
  192.5 1.5 collective-permute-start.2
  194.0 93.0 %attention.6.refs_0_ = bf16[6,1,512,4096]{3,2,1,0:T(8,128)(2,1)} custom-call(f32[1,4096]{1,0:T(1,128)} %norm_ref.11, bf16[512,4096]{1,0:T(8,128)(2,1)} %collective-permute-done.5.y_hbm, bf16[4,4096,512]{2,1,0:T(8,128)(2,1)} %regroup.3.wq_hbm, bf16[4,4096,512]{2,1,0:T(8,128)(2,1)} %regroup.4.wk_hbm, bf16[4,4096,512]{2,1,0:T(8,128)(2,1)} %collective-permute-done.6.oq_hbm, ...), custom_call_target="tpu_custom_call" | custom-call | flops 68719476736 | bytes 134217728 | tf_op jit(solution)/shard_map/attention/pallas_call | solution.py:301
  287.0 0.0 collective-permute-done.4.y_hbm
  287.0 93.5 %attention.7.refs_0_ = bf16[6,1,512,4096]{3,2,1,0:T(8,128)(2,1)} custom-call(f32[1,4096]{1,0:T(1,128)} %norm_ref.11, bf16[512,4096]{1,0:T(8,128)(2,1)} %collective-permute-done.4.y_hbm, bf16[4,4096,512]{2,1,0:T(8,128)(2,1)} %regroup.3.wq_hbm, bf16[4,4096,512]{2,1,0:T(8,128)(2,1)} %regroup.4.wk_hbm, ...), custom_call_target="tpu_custom_call", output_to_operand_aliasing={{}: (8, {})} | custom-call | flops 68719476736 | bytes 134217728 | tf_op jit(solution)/shard_map/attention/pallas_call | solution.py:301
  380.5 0.0 collective-permute-done.3.y_hbm
  380.5 93.0 %attention.8.refs_0_ = bf16[6,1,512,4096]{3,2,1,0:T(8,128)(2,1)} custom-call(f32[1,4096]{1,0:T(1,128)} %norm_ref.11, bf16[512,4096]{1,0:T(8,128)(2,1)} %collective-permute-done.3.y_hbm, bf16[4,4096,512]{2,1,0:T(8,128)(2,1)} %regroup.3.wq_hbm, bf16[4,4096,512]{2,1,0:T(8,128)(2,1)} %regroup.4.wk_hbm, ...), custom_call_target="tpu_custom_call", output_to_operand_aliasing={{}: (8, {})} | custom-call | flops 68719476736 | bytes 134217728 | tf_op jit(solution)/shard_map/attention/pallas_call | solution.py:301
  473.5 129.9 %collective-permute-done.2.y_hbm = bf16[512,4096]{1,0:T(8,128)(2,1)} collective-permute-done((bf16[512,4096]{1,0:T(8,128)(2,1)}, bf16[512,4096]{1,0:T(8,128)(2,1)}, u32[]{:S(2)}, u32[]{:S(2)}) %collective-permute-start.2) | collective-permute-done | bytes 4194336 | tf_op jit(solution)/shard_map/ppermute | solution.py:356
  603.4 93.0 %attention.9.refs_0_ = bf16[6,1,512,4096]{3,2,1,0:T(8,128)(2,1)} custom-call(f32[1,4096]{1,0:T(1,128)} %norm_ref.11, bf16[512,4096]{1,0:T(8,128)(2,1)} %collective-permute-done.2.y_hbm, bf16[4,4096,512]{2,1,0:T(8,128)(2,1)} %regroup.3.wq_hbm, bf16[4,4096,512]{2,1,0:T(8,128)(2,1)} %regroup.4.wk_hbm, ...), custom_call_target="tpu_custom_call", output_to_operand_aliasing={{}: (8, {})} | custom-call | flops 68719476736 | bytes 134217728 | tf_op jit(solution)/shard_map/attention/pallas_call | solution.py:301
  696.5 0.0 collective-permute-done.1.y_hbm
  696.5 93.1 %attention.10.refs_0_ = bf16[6,1,512,4096]{3,2,1,0:T(8,128)(2,1)} custom-call(f32[1,4096]{1,0:T(1,128)} %norm_ref.11, bf16[512,4096]{1,0:T(8,128)(2,1)} %collective-permute-done.1.y_hbm, bf16[4,4096,512]{2,1,0:T(8,128)(2,1)} %regroup.3.wq_hbm, bf16[4,4096,512]{2,1,0:T(8,128)(2,1)} %regroup.4.wk_hbm, ...), custom_call_target="tpu_custom_call", output_to_operand_aliasing={{}: (8, {})} | custom-call | flops 68719476736 | bytes 134217728 | tf_op jit(solution)/shard_map/attention/pallas_call | solution.py:301
  789.6 0.0 collective-permute-done.y_hbm
  789.6 93.0 %attention.11 = bf16[6,1,512,4096]{3,2,1,0:T(8,128)(2,1)} custom-call(f32[1,4096]{1,0:T(1,128)} %norm_ref.11, bf16[512,4096]{1,0:T(8,128)(2,1)} %collective-permute-done.y_hbm, bf16[4,4096,512]{2,1,0:T(8,128)(2,1)} %regroup.3.wq_hbm, bf16[4,4096,512]{2,1,0:T(8,128)(2,1)} %regroup.4.wk_hbm, ...), custom_call_target="tpu_custom_call", output_to_operand_aliasing={{}: (8, {})} | custom-call | flops 68719476736 | bytes 134217728 | tf_op jit(solution)/shard_map/attention/pallas_call | solution.py:301
Async XLA Ops:
  59.7 131.3 %collective-permute-start.7 = (bf16[4,4096,512]{2,1,0:T(8,128)(2,1)}, bf16[4,4096,512]{2,1,0:T(8,128)(2,1)}, u32[]{:S(2)}, u32[]{:S(2)}) collective-permute-start(bf16[4,4096,512]{2,1,0:T(8,128)(2,1)} %regroup.4.wk_hbm), channel_id=1, source_target_pairs={{0,1},{1,0},{2,3},{3,2},{4,5},{5,4},{6,7},{7,6}} | collective-permute-start | bytes 50331656 | tf_op jit(solution)/shard_map/ppermute | solution.py:366
  59.8 132.7 %collective-permute-start.6 = (bf16[4,4096,512]{2,1,0:T(8,128)(2,1)}, bf16[4,4096,512]{2,1,0:T(8,128)(2,1)}, u32[]{:S(2)}, u32[]{:S(2)}) collective-permute-start(bf16[4,4096,512]{2,1,0:T(8,128)(2,1)} %regroup.3.wq_hbm), channel_id=1, source_target_pairs={{0,1},{1,0},{2,3},{3,2},{4,5},{5,4},{6,7},{7,6}} | collective-permute-start | bytes 50331656 | tf_op jit(solution)/shard_map/ppermute | solution.py:366
  60.2 128.8 %collective-permute-start.5 = (bf16[512,4096]{1,0:T(8,128)(2,1)}, bf16[512,4096]{1,0:T(8,128)(2,1)}, u32[]{:S(2)}, u32[]{:S(2)}) collective-permute-start(bf16[512,4096]{1,0:T(8,128)(2,1)} %combine.3), channel_id=1, source_target_pairs={{0,2},{2,4},{4,6},{6,0},{1,3},{3,5},{5,7},{7,1}} | collective-permute-start | bytes 12582920 | tf_op jit(solution)/shard_map/ppermute | solution.py:356
  139.2 147.8 %collective-permute-start.4 = (bf16[512,4096]{1,0:T(8,128)(2,1)}, bf16[512,4096]{1,0:T(8,128)(2,1)}, u32[]{:S(2)}, u32[]{:S(2)}) collective-permute-start(bf16[512,4096]{1,0:T(8,128)(2,1)} %get-tuple-element.37), channel_id=1, source_target_pairs={{0,2},{2,4},{4,6},{6,0},{1,3},{3,5},{5,7},{7,1}} | collective-permute-start | bytes 12582920 | tf_op jit(solution)/shard_map/ppermute | solution.py:356
  140.7 239.8 %collective-permute-start.3 = (bf16[512,4096]{1,0:T(8,128)(2,1)}, bf16[512,4096]{1,0:T(8,128)(2,1)}, u32[]{:S(2)}, u32[]{:S(2)}) collective-permute-start(bf16[512,4096]{1,0:T(8,128)(2,1)} %get-tuple-element.32), channel_id=1, source_target_pairs={{0,2},{2,4},{4,6},{6,0},{1,3},{3,5},{5,7},{7,1}} | collective-permute-start | bytes 12582920 | tf_op jit(solution)/shard_map/ppermute | solution.py:356
  189.0 600.6 %collective-permute-start = (bf16[512,4096]{1,0:T(8,128)(2,1)}, bf16[512,4096]{1,0:T(8,128)(2,1)}, u32[]{:S(2)}, u32[]{:S(2)}) collective-permute-start(bf16[512,4096]{1,0:T(8,128)(2,1)} %get-tuple-element.34), channel_id=1, source_target_pairs={{0,2},{2,4},{4,6},{6,0},{1,3},{3,5},{5,7},{7,1}} | collective-permute-start | bytes 12582920 | tf_op jit(solution)/shard_map/ppermute | solution.py:356
  191.0 505.5 %collective-permute-start.1 = (bf16[512,4096]{1,0:T(8,128)(2,1)}, bf16[512,4096]{1,0:T(8,128)(2,1)}, u32[]{:S(2)}, u32[]{:S(2)}) collective-permute-start(bf16[512,4096]{1,0:T(8,128)(2,1)} %get-tuple-element.35), channel_id=1, source_target_pairs={{0,2},{2,4},{4,6},{6,0},{1,3},{3,5},{5,7},{7,1}} | collective-permute-start | bytes 12582920 | tf_op jit(solution)/shard_map/ppermute | solution.py:356
  192.5 411.0 %collective-permute-start.2 = (bf16[512,4096]{1,0:T(8,128)(2,1)}, bf16[512,4096]{1,0:T(8,128)(2,1)}, u32[]{:S(2)}, u32[]{:S(2)}) collective-permute-start(bf16[512,4096]{1,0:T(8,128)(2,1)} %get-tuple-element.36), channel_id=1, source_target_pairs={{0,2},{2,4},{4,6},{6,0},{1,3},{3,5},{5,7},{7,1}} | collective-permute-start | bytes 12582920 | tf_op jit(solution)/shard_map/ppermute | solution.py:356
